TPU v7x, 32 devices: a whole 2x2x4 slice. The times are simulated.
32 devices in a mesh: blk: 8 (over z, x), lane: 4 (over y, core).
Axes of the slice: x: 2, y: 2, z: 4, core: 2. Of those that a mesh axis runs over, the one named last changes fastest.
Arguments:
- left_factor: bfloat16 [4096, 512], P('blk'), may hold values from -6 to 6
- right_factor: bfloat16 [4, 4096, 512], P('lane', 'blk'), may hold values from -6 to 6
- observed: bfloat16 [4, 4, 512, 4096], P('lane', None, None, 'blk'), may hold values from -6 to 6
- row_codes: int32 [4096], P('blk'), may hold values from 0 to 1073741823
- shift_codes: int32 [4, 4, 4096], P('lane', None, 'blk'), may hold values from 0 to 29
Outputs:
- left_out: bfloat16 [4096, 512], P('blk')
- right_out: bfloat16 [4, 4096, 512], P('lane', 'blk')
Inputs may be any that keep to these rules, and one draw needn't show every extreme that they name: `row_codes`: each row's word carries thirty independent sampling bits. `shift_codes`: A bit number for each lane, cycle step and visited tile entry column.
All inputs are finite; a program needn't handle non-finite values.
Results may differ from a plain program's by a relative error of at most 0.013.
Values may be sent and summed in bfloat16 or wider, within the bound.
A program may use at most 64 MiB of HBM per device.

v0:
```python
import functools
import math

import jax
import jax.numpy as jnp
from jax import lax
from jax.experimental import pallas as pl
from jax.experimental.pallas import tpu as pltpu
from jax.sharding import PartitionSpec as P

step_right = 0.25
step_left = 0.1

CHUNKS = 4
WIDTH = 128
PARTS = 2
PIECES = 4
MESH = pl.DeviceIdType.MESH


def kernel(
    blocks, lanes,
    left_hbm, right_hbm, obs_hbm, codes_hbm, shift_hbm,
    left_out, right_out,
    left, visited, updated, obs, codes, shift, turned, errors, grad, pair_out, pair_in, peer_out, peer_in, result,
    load_sem, send_sem, recv_sem, pair_send, pair_recv, peer_send, peer_recv, last_send, last_recv, out_sem,
):
    steps, cols, rows = obs.shape
    rank = left.shape[1]
    scale = 1.0 / math.sqrt(rank)
    size = cols // CHUNKS
    half = rows // 2
    part = half // PIECES
    width = turned.shape[1]
    blk = lax.axis_index("blk")
    lane = lax.axis_index("lane")
    ahead = lax.rem(blk + 1, blocks)
    behind = lax.rem(blk + blocks - 1, blocks)
    side = lax.rem(lane, 2)
    pair = lane + 1 - 2 * side
    peers = [lax.rem(lane + 2 * hop, lanes) for hop in range(1, lanes // 2)]
    mine = pl.multiple_of(side * half, half)
    other = pl.multiple_of((1 - side) * half, half)

    barrier = pltpu.get_barrier_semaphore()
    pl.semaphore_signal(barrier, inc=1, device_id={"blk": behind}, device_id_type=MESH)
    for friend in [pair] + peers:
        pl.semaphore_signal(barrier, inc=1, device_id={"lane": friend}, device_id_type=MESH)

    loads = [
        pltpu.make_async_copy(shift_hbm, shift, load_sem.at[0]),
        pltpu.make_async_copy(codes_hbm, codes, load_sem.at[1]),
        pltpu.make_async_copy(right_hbm.at[0], visited.at[0], load_sem.at[2]),
        pltpu.make_async_copy(left_hbm, left, load_sem.at[3]),
    ]
    for s in range(steps):
        loads.append(pltpu.make_async_copy(obs_hbm.at[0, s], obs.at[s], load_sem.at[4 + s]))
    for copy in loads[:5]:
        copy.start()

    def hop(s, k):
        span = pl.ds(pl.multiple_of(k * size, size), size)
        return pltpu.make_async_remote_copy(
            src_ref=updated.at[s, span],
            dst_ref=visited.at[s + 1, span],
            send_sem=send_sem.at[s, k],
            recv_sem=recv_sem.at[s, k],
            device_id={"blk": ahead},
            device_id_type=MESH,
        )

    def turn(s):
        for first in range(0, cols, width):
            span = pl.ds(first, width)
            turned[span, :] = jnp.transpose(jnp.broadcast_to(shift[0, pl.ds(s, 1), span], (width, width)))

    def error_of(s, k):
        span = pl.ds(pl.multiple_of(k * size, size), size)
        shifts = jnp.concatenate([turned[span, :]] * (rows // width), axis=1)
        seen = (jnp.right_shift(codes[...], shifts) & 1) == 1
        predicted = lax.dot_general(
            visited[s, span, :], left[...], (((1,), (1,)), ((), ())), preferred_element_type=jnp.float32
        )
        error = predicted * scale - obs[s, span, :].astype(jnp.float32)
        return jnp.where(seen, error, 0.0).astype(jnp.bfloat16)

    def stepped(error, block):
        move = jnp.dot(error, left[...], preferred_element_type=jnp.float32)
        return (block.astype(jnp.float32) - step_right * scale * move).astype(jnp.bfloat16)

    def add_left(error, block):
        grad[...] += lax.dot_general(
            error, block, (((0,), (0,)), ((), ())), preferred_element_type=jnp.float32
        )

    def visit(s, k, before_send=None):
        span = pl.ds(pl.multiple_of(k * size, size), size)
        if s > 0:
            hop(s - 1, k).wait_recv()
        error = error_of(s, k)
        block = visited[s, span, :]
        updated[s, span, :] = stepped(error, block)
        if before_send is not None:
            before_send()
        hop(s, k).start()
        add_left(error, block)

    grad[...] = jnp.zeros_like(grad)
    loads[0].wait()
    turn(0)
    for copy in loads[1:5]:
        copy.wait()
    visit(0, 0, lambda: pl.semaphore_wait(barrier, 2 + len(peers)))
    for copy in loads[5:]:
        copy.start()
    for s in range(steps - 1):
        if s > 0:
            loads[4 + s].wait()
            turn(s)
        pl.loop(1 if s == 0 else 0, CHUNKS)(functools.partial(visit, s))

    last = steps - 1
    loads[4 + last].wait()
    turn(last)

    @pl.loop(0, CHUNKS - 1)
    def _(k):
        span = pl.ds(pl.multiple_of(k * size, size), size)
        hop(last - 1, k).wait_recv()
        error = error_of(last, k)
        errors[span, :] = error
        add_left(error, visited[last, span, :])

    tail = pl.ds((CHUNKS - 1) * size, size)
    hop(last - 1, CHUNKS - 1).wait_recv()
    errors[tail, :] = error_of(last, CHUNKS - 1)

    def finish(first):
        span = pl.ds(first, half)
        return grad[span, :] + lax.dot_general(
            errors[tail, span], visited[last, tail, :], (((0,), (0,)), ((), ())), preferred_element_type=jnp.float32
        )

    def swap(q):
        span = pl.ds(q * part, part)
        return pltpu.make_async_remote_copy(
            src_ref=pair_out.at[span], dst_ref=pair_in.at[span],
            send_sem=pair_send.at[q], recv_sem=pair_recv.at[q],
            device_id={"lane": pair}, device_id_type=MESH,
        )

    def cross(m, q):
        span = pl.ds(q * part, part)
        return pltpu.make_async_remote_copy(
            src_ref=peer_out.at[span], dst_ref=peer_in.at[m, span],
            send_sem=peer_send.at[m, q], recv_sem=peer_recv.at[m, q],
            device_id={"lane": peers[m]}, device_id_type=MESH,
        )

    def share(q):
        span = pl.ds(pl.multiple_of(mine + q * part, part), part)
        return pltpu.make_async_remote_copy(
            src_ref=result.at[span], dst_ref=result.at[span],
            send_sem=last_send.at[q], recv_sem=last_recv.at[q],
            device_id={"lane": pair}, device_id_type=MESH,
        )

    pair_out[...] = finish(other).astype(jnp.bfloat16)
    for q in range(PIECES):
        swap(q).start()
    grad[pl.ds(mine, half), :] = finish(mine)
    for q in range(PIECES):
        span = pl.ds(q * part, part)
        swap(q).wait_recv()
        peer_out[span, :] = (
            grad[pl.ds(pl.multiple_of(mine + q * part, part), part), :] + pair_in[span, :].astype(jnp.float32)
        ).astype(jnp.bfloat16)
        for m in range(len(peers)):
            cross(m, q).start()

    @pl.loop(0, CHUNKS)
    def _(k):
        span = pl.ds(pl.multiple_of(k * size, size), size)
        updated[last, span, :] = stepped(errors[span, :], visited[last, span, :])

    outs = [
        pltpu.make_async_copy(updated.at[last], right_out.at[0], out_sem.at[0]),
        pltpu.make_async_copy(result.at[pl.ds(mine, half)], left_out.at[pl.ds(mine, half)], out_sem.at[1]),
        pltpu.make_async_copy(result.at[pl.ds(other, half)], left_out.at[pl.ds(other, half)], out_sem.at[2]),
    ]
    outs[0].start()
    for s in range(steps - 1):
        @pl.loop(0, CHUNKS)
        def _(k):
            hop(s, k).wait_send()

    for q in range(PIECES):
        span = pl.ds(q * part, part)
        here = pl.ds(pl.multiple_of(mine + q * part, part), part)
        total = peer_out[span, :].astype(jnp.float32)
        for m in range(len(peers)):
            cross(m, q).wait_recv()
            total = total + peer_in[m, span, :].astype(jnp.float32)
        result[here, :] = (left[here, :].astype(jnp.float32) - step_left * scale * total).astype(jnp.bfloat16)
        share(q).start()
    outs[1].start()
    for q in range(PIECES):
        share(q).wait_recv()
    outs[2].start()
    for q in range(PIECES):
        swap(q).wait_send()
        for m in range(len(peers)):
            cross(m, q).wait_send()
        share(q).wait_send()
    for copy in outs:
        copy.wait()


def place(left_from, right_from, left_to, right_to, held, in_sem, out_sem):
    pairs = [(left_from, left_to), (right_from.at[0], right_to.at[0])]
    rows = left_from.shape[0] // PARTS
    moves = []
    for which, (source, target) in enumerate(pairs):
        for p in range(PARTS):
            span = pl.ds(p * rows, rows)
            moves.append((
                pltpu.make_async_copy(source.at[span], held.at[which, span], in_sem.at[which, p]),
                pltpu.make_async_copy(held.at[which, span], target.at[span], out_sem.at[which, p]),
            ))
    for inward, _ in moves:
        inward.start()
    for inward, outward in moves:
        inward.wait()
        outward.start()
    for _, outward in moves:
        outward.wait()


def solution(mesh):
    blocks = mesh.shape["blk"]
    lanes = mesh.shape["lane"]

    def local(left_factor, right_factor, observed, row_codes, shift_codes):
        rows, rank = left_factor.shape
        _, steps, cols, _ = observed.shape
        bf16, f32 = jnp.bfloat16, jnp.float32
        dma = pltpu.SemaphoreType.DMA
        hbm = pl.BlockSpec(memory_space=pltpu.HBM)
        others = lanes // 2 - 1
        shapes = (
            jax.ShapeDtypeStruct((rows, rank), bf16),
            jax.ShapeDtypeStruct((1, cols, rank), bf16),
        )
        results = pl.pallas_call(
            functools.partial(kernel, blocks, lanes),
            out_shape=shapes,
            in_specs=[hbm] * 5,
            out_specs=(hbm, hbm),
            scratch_shapes=[
                pltpu.VMEM((rows, rank), bf16),
                pltpu.VMEM((steps, cols, rank), bf16),
                pltpu.VMEM((steps, cols, rank), bf16),
                pltpu.VMEM((steps, cols, rows), bf16),
                pltpu.VMEM((1, rows), jnp.int32),
                pltpu.VMEM((1, steps, cols), jnp.int32),
                pltpu.VMEM((cols, WIDTH), jnp.int32),
                pltpu.VMEM((cols, rows), bf16),
                pltpu.VMEM((rows, rank), f32),
                pltpu.VMEM((rows // 2, rank), bf16),
                pltpu.VMEM((rows // 2, rank), bf16),
                pltpu.VMEM((rows // 2, rank), bf16),
                pltpu.VMEM((others, rows // 2, rank), bf16),
                pltpu.VMEM((rows, rank), bf16),
                dma((4 + steps,)),
                dma((steps - 1, CHUNKS)),
                dma((steps - 1, CHUNKS)),
                dma((PIECES,)),
                dma((PIECES,)),
                dma((others, PIECES)),
                dma((others, PIECES)),
                dma((PIECES,)),
                dma((PIECES,)),
                dma((3,)),
            ],
            compiler_params=pltpu.CompilerParams(
                collective_id=0, has_side_effects=True, vmem_limit_bytes=67043328
            ),
        )(
            left_factor, right_factor, observed,
            row_codes.reshape(1, rows), shift_codes,
        )
        return pl.pallas_call(
            place,
            out_shape=shapes,
            in_specs=[hbm] * 2,
            out_specs=(hbm, hbm),
            scratch_shapes=[pltpu.VMEM((2, max(rows, cols), rank), bf16), dma((2, PARTS)), dma((2, PARTS))],
            compiler_params=pltpu.CompilerParams(vmem_limit_bytes=67043328),
        )(*results)

    in_specs = (
        P("blk", None),
        P("lane", "blk", None),
        P("lane", None, None, "blk"),
        P("blk"),
        P("lane", None, "blk"),
    )
    out_specs = (P("blk", None), P("lane", "blk", None))
    return jax.shard_map(local, mesh=mesh, in_specs=in_specs, out_specs=out_specs, check_vma=False)
```

profile of v0, /device:TPU:0, one launch (start us, length us, event | category | flops | bytes accessed | tf_op | source)
XLA Modules:
  0.0 56.3 jit_solution(16462920265520179514)
XLA Ops:
  0.6 53.7 %shard_map.68 = (bf16[512,512]{1,0:T(8,128)(2,1)}, bf16[1,512,512]{2,1,0:T(8,128)(2,1)}) custom-call(bf16[512,512]{1,0:T(8,128)(2,1)} %left_hbm.1, bf16[1,512,512]{2,1,0:T(8,128)(2,1)} %right_hbm.1, bf16[1,4,512,512]{3,2,1,0:T(8,128)(2,1)} %obs_hbm.1, s32[1,512]{1,0:T(1,128)} %bitcast.1, s32[1,4,512]{2,1,0:T(4,128)} %shift_hbm.1), custom_call_target="tpu_custom_call" | custom-call | tf_op jit(solution)/shard_map/pallas_call | solution.py:254
  54.3 2.0 %shard_map.69 = (bf16[512,512]{1,0:T(8,128)(2,1)}, bf16[1,512,512]{2,1,0:T(8,128)(2,1)}) custom-call(bf16[512,512]{1,0:T(8,128)(2,1)} %get-tuple-element.4.left_from, bf16[1,512,512]{2,1,0:T(8,128)(2,1)} %get-tuple-element.5.right_from), custom_call_target="tpu_custom_call" | custom-call | tf_op jit(solution)/shard_map/pallas_call | solution.py:292
where the time goes:
time: 56.5 us; the launch traced here: 56.3 us
  Pallas kernels  55.7 us (99%)
  between operations  0.64 us (1%)
    pallas_call x1, Pallas kernels, local(): pl.pallas_call(functools.partial(kernel, blocks, lanes), out_shape=shapes...  53.7 us
    pallas_call x1, Pallas kernels, local(): pl.pallas_call(place, out_shape=shapes, in_specs=[hbm] * 2, out_specs=(hb...  1.98 us

commit v1 on v0

v1 whole, which is shorter than its diff:
```python
import functools
import math

import jax
import jax.numpy as jnp
from jax import lax
from jax.experimental import pallas as pl
from jax.experimental.pallas import tpu as pltpu
from jax.sharding import PartitionSpec as P

step_right = 0.25
step_left = 0.1

CHUNKS = 4
WIDTH = 128
PARTS = 2
PIECES = 4
SUBS = 2
GUEST = 1
MESH = pl.DeviceIdType.MESH


def kernel(
    blocks, lanes,
    left_hbm, right_hbm, obs_hbm, codes_hbm, shift_hbm,
    left_out, right_out,
    left, left_g, first, inner, hop_out, hop_in, turn_out, turn_in, final,
    obs, obs_g, codes, codes_g, shift, shift_g, turned, errs,
    grad, grad_g, back_out, back_in, ret_out, ret_in, pair_out, pair_in, peer_out, peer_in, result,
    load_sem, tile_send, tile_recv, table_send, table_recv, share_send, share_recv,
    peer_share_send, peer_share_recv, pair_share_send, pair_share_recv,
    hop_send, hop_recv, turn_send, turn_recv, back_send, back_recv, ret_send, ret_recv,
    swap_send, swap_recv, cross_send, cross_recv, last_send, last_recv, out_sem,
):
    steps, cols, rows = errs.shape
    rank = left.shape[1]
    scale = 1.0 / math.sqrt(rank)
    size = cols // CHUNKS
    half = rows // 2
    part = half // PIECES
    own = rows // lanes
    sub = own // SUBS
    width = turned.shape[2]
    others = lanes // 2 - 1
    blk = lax.axis_index("blk")
    lane = lax.axis_index("lane")
    odd = lax.rem(blk, 2)
    partner = blk + 1 - 2 * odd
    ahead = lax.rem(blk + 1, blocks)
    behind = lax.rem(blk + blocks - 1, blocks)
    ahead2 = lax.rem(blk + 2, blocks)
    behind2 = lax.rem(blk + blocks - 2, blocks)
    side = lax.rem(lane, 2)
    pair = lane + 1 - 2 * side
    peers = [lax.rem(lane + 2 * hop, lanes) for hop in range(1, lanes // 2)]
    sources = [lax.rem(lane + lanes - 2 * hop, lanes) for hop in range(1, lanes // 2)]
    mine = pl.multiple_of(side * half, half)
    other = pl.multiple_of((1 - side) * half, half)

    barrier = pltpu.get_barrier_semaphore()
    for target in (partner, behind, behind2):
        pl.semaphore_signal(barrier, inc=1, device_id={"blk": target}, device_id_type=MESH)
    for friend in [pair] + peers:
        pl.semaphore_signal(barrier, inc=1, device_id={"lane": friend}, device_id_type=MESH)

    def remote(source, target, send, recv, **place):
        return pltpu.make_async_remote_copy(
            src_ref=source, dst_ref=target, send_sem=send, recv_sem=recv,
            device_id=place, device_id_type=MESH,
        )

    def chunk(k):
        return pl.ds(pl.multiple_of(k * size, size), size)

    natural = [s for s in range(steps) if s != GUEST]
    loads = [
        pltpu.make_async_copy(shift_hbm, shift, load_sem.at[0]),
        pltpu.make_async_copy(codes_hbm, codes, load_sem.at[1]),
        pltpu.make_async_copy(right_hbm.at[0], first, load_sem.at[2]),
        pltpu.make_async_copy(left_hbm, left, load_sem.at[3]),
    ]
    for n, s in enumerate(natural):
        loads.append(pltpu.make_async_copy(obs_hbm.at[0, s], obs.at[n], load_sem.at[4 + n]))
    for copy in loads:
        copy.start()

    def piece(owner, u):
        return pl.ds(pl.multiple_of(owner * own + u * sub, sub), sub)

    def lend(u):
        span = piece(lane, u)
        return remote(left_hbm.at[span], left_g.at[span], share_send.at[u], share_recv.at[u], blk=partner)

    def lend_peer(m, u):
        span = piece(lane, u)
        return remote(left_g.at[span], left_g.at[span], peer_share_send.at[m, u], peer_share_recv.at[m, u], lane=peers[m])

    def lend_pair(m, u):
        span = piece(lane if m == 0 else sources[m - 1], u)
        return remote(left_g.at[span], left_g.at[span], pair_share_send.at[m, u], pair_share_recv.at[m, u], lane=pair)

    def give(k):
        span = chunk(k)
        return remote(obs_hbm.at[0, GUEST, span], obs_g.at[span], tile_send.at[k], tile_recv.at[k], blk=partner)

    tables = [
        remote(codes_hbm, codes_g, table_send.at[0], table_recv.at[0], blk=partner),
        remote(shift_hbm, shift_g, table_send.at[1], table_recv.at[1], blk=partner),
    ]

    def hop(k):
        span = chunk(k)
        return remote(hop_out.at[span], hop_in.at[span], hop_send.at[k], hop_recv.at[k], blk=ahead2)

    def cross_over(k):
        span = chunk(k)
        return remote(turn_out.at[span], turn_in.at[span], turn_send.at[k], turn_recv.at[k], blk=ahead)

    def turn(s, table):
        for start in range(0, cols, width):
            span = pl.ds(start, width)
            turned[s, span, :] = jnp.transpose(jnp.broadcast_to(table[0, pl.ds(s, 1), span], (width, width)))

    def error_of(k, s, block, factor, words, target):
        span = chunk(k)
        shifts = jnp.concatenate([turned[s, span, :]] * (rows // width), axis=1)
        seen = (jnp.right_shift(words[...], shifts) & 1) == 1
        predicted = lax.dot_general(
            block, factor[...], (((1,), (1,)), ((), ())), preferred_element_type=jnp.float32
        )
        error = predicted * scale - target[span, :].astype(jnp.float32)
        return jnp.where(seen, error, 0.0).astype(jnp.bfloat16)

    def stepped(error, block, factor):
        move = jnp.dot(error, factor[...], preferred_element_type=jnp.float32)
        return (block.astype(jnp.float32) - step_right * scale * move).astype(jnp.bfloat16)

    def tile(k, s, source, target, guest=False):
        span = chunk(k)
        block = source[span, :]
        if guest:
            factor, words, wanted = left_g, codes_g, obs_g
        else:
            factor, words, wanted = left, codes, obs.at[natural.index(s)]
        error = error_of(k, s, block, factor, words, wanted)
        errs[s, span, :] = error
        target[span, :] = stepped(error, block, factor)

    def outer(error, block):
        return lax.dot_general(error, block, (((0,), (0,)), ((), ())), preferred_element_type=jnp.float32)

    loads[0].wait()
    turn(0, shift)
    pl.semaphore_wait(barrier, 3 + 1 + len(peers))
    for u in range(SUBS):
        lend(u).start()
    for copy in tables:
        copy.start()
    for k in range(CHUNKS):
        give(k).start()
    for copy in loads[1:5]:
        copy.wait()

    def relay():
        for u in range(SUBS):
            lend(u).wait_recv()
            for m in range(others):
                lend_peer(m, u).start()
            lend_pair(0, u).start()

    def gather():
        for u in range(SUBS):
            for m in range(others):
                lend_peer(m, u).wait_recv()
                lend_pair(1 + m, u).start()
        for copy in tables:
            copy.wait_recv()
        turn(GUEST, shift_g)
        for m in range(1 + others):
            for u in range(SUBS):
                lend_pair(m, u).wait_recv()

    @pl.when(odd == 0)
    def _():
        pl.loop(0, CHUNKS)(lambda k: tile(k, 0, first, inner))
        relay()
        grad[...] = outer(errs[0], first[...])
        turn(2, shift)
        turn(3, shift)
        gather()

        @pl.loop(0, CHUNKS)
        def _(k):
            give(k).wait_recv()
            tile(k, 1, inner, hop_out, guest=True)
            hop(k).start()

        grad_g[...] = outer(errs[1], inner[...])
        loads[5].wait()

        @pl.loop(0, CHUNKS)
        def _(k):
            hop(k).wait_recv()
            tile(k, 2, hop_in, turn_out)
            cross_over(k).start()

        grad[...] += outer(errs[2], hop_in[...])

    @pl.when(odd == 1)
    def _():
        @pl.loop(0, CHUNKS)
        def _(k):
            tile(k, 0, first, hop_out)
            hop(k).start()

        relay()
        grad[...] = outer(errs[0], first[...])
        turn(2, shift)
        turn(3, shift)
        gather()
        loads[5].wait()

        @pl.loop(0, CHUNKS)
        def _(k):
            give(k).wait_recv()
            hop(k).wait_recv()
            tile(k, 1, hop_in, inner, guest=True)
            tile(k, 2, inner, turn_out)
            cross_over(k).start()

        grad_g[...] = outer(errs[1], hop_in[...])
        grad[...] += outer(errs[2], inner[...])

    back = remote(back_out, back_in, back_send.at[0], back_recv.at[0], lane=pair)
    back_out[...] = grad_g[pl.ds(other, half), :].astype(jnp.bfloat16)
    back.start()

    def give_back(q):
        span = pl.ds(q * part, part)
        return remote(ret_out.at[span], ret_in.at[span], ret_send.at[q], ret_recv.at[q], blk=partner)

    loads[6].wait()
    last = steps - 1

    @pl.loop(0, CHUNKS - 1)
    def _(k):
        cross_over(k).wait_recv()
        tile(k, last, turn_in, final)

    early = (CHUNKS - 1) * size
    grad[...] += outer(errs[last, pl.ds(0, early)], turn_in[pl.ds(0, early)])
    back.wait_recv()
    ret_out[...] = (grad_g[pl.ds(mine, half), :] + back_in[...].astype(jnp.float32)).astype(jnp.bfloat16)
    for q in range(PIECES):
        give_back(q).start()

    tail = pl.ds(early, size)
    cross_over(CHUNKS - 1).wait_recv()
    errs[last, tail, :] = error_of(CHUNKS - 1, last, turn_in[tail, :], left, codes, obs.at[natural.index(last)])

    def finish(start):
        span = pl.ds(start, half)
        return grad[span, :] + outer(errs[last, tail, span], turn_in[tail, :])

    def swap(q):
        span = pl.ds(q * part, part)
        return remote(pair_out.at[span], pair_in.at[span], swap_send.at[q], swap_recv.at[q], lane=pair)

    def cross(m, q):
        span = pl.ds(q * part, part)
        return remote(peer_out.at[span], peer_in.at[m, span], cross_send.at[m, q], cross_recv.at[m, q], lane=peers[m])

    def share(q):
        span = pl.ds(pl.multiple_of(mine + q * part, part), part)
        return remote(result.at[span], result.at[span], last_send.at[q], last_recv.at[q], lane=pair)

    pair_out[...] = finish(other).astype(jnp.bfloat16)
    for q in range(PIECES):
        swap(q).start()
    grad[pl.ds(mine, half), :] = finish(mine)
    for q in range(PIECES):
        span = pl.ds(q * part, part)
        swap(q).wait_recv()
        give_back(q).wait_recv()
        peer_out[span, :] = (
            grad[pl.ds(pl.multiple_of(mine + q * part, part), part), :]
            + pair_in[span, :].astype(jnp.float32)
            + ret_in[span, :].astype(jnp.float32)
        ).astype(jnp.bfloat16)
        for m in range(len(peers)):
            cross(m, q).start()

    final[tail, :] = stepped(errs[last, tail, :], turn_in[tail, :], left)

    outs = [
        pltpu.make_async_copy(final, right_out.at[0], out_sem.at[0]),
        pltpu.make_async_copy(result.at[pl.ds(mine, half)], left_out.at[pl.ds(mine, half)], out_sem.at[1]),
        pltpu.make_async_copy(result.at[pl.ds(other, half)], left_out.at[pl.ds(other, half)], out_sem.at[2]),
    ]
    outs[0].start()
    for u in range(SUBS):
        lend(u).wait_send()
        for m in range(others):
            lend_peer(m, u).wait_send()
        for m in range(1 + others):
            lend_pair(m, u).wait_send()
    for copy in tables:
        copy.wait_send()

    @pl.loop(0, CHUNKS)
    def _(k):
        give(k).wait_send()
        hop(k).wait_send()
        cross_over(k).wait_send()

    back.wait_send()

    for q in range(PIECES):
        span = pl.ds(q * part, part)
        here = pl.ds(pl.multiple_of(mine + q * part, part), part)
        total = peer_out[span, :].astype(jnp.float32)
        for m in range(len(peers)):
            cross(m, q).wait_recv()
            total = total + peer_in[m, span, :].astype(jnp.float32)
        result[here, :] = (left[here, :].astype(jnp.float32) - step_left * scale * total).astype(jnp.bfloat16)
        share(q).start()
    outs[1].start()
    for q in range(PIECES):
        share(q).wait_recv()
    outs[2].start()
    for q in range(PIECES):
        give_back(q).wait_send()
        swap(q).wait_send()
        for m in range(len(peers)):
            cross(m, q).wait_send()
        share(q).wait_send()
    for copy in outs:
        copy.wait()


def place(left_from, right_from, left_to, right_to, held, in_sem, out_sem):
    pairs = [(left_from, left_to), (right_from.at[0], right_to.at[0])]
    rows = left_from.shape[0] // PARTS
    moves = []
    for which, (source, target) in enumerate(pairs):
        for p in range(PARTS):
            span = pl.ds(p * rows, rows)
            moves.append((
                pltpu.make_async_copy(source.at[span], held.at[which, span], in_sem.at[which, p]),
                pltpu.make_async_copy(held.at[which, span], target.at[span], out_sem.at[which, p]),
            ))
    for inward, _ in moves:
        inward.start()
    for inward, outward in moves:
        inward.wait()
        outward.start()
    for _, outward in moves:
        outward.wait()


def solution(mesh):
    blocks = mesh.shape["blk"]
    lanes = mesh.shape["lane"]

    def local(left_factor, right_factor, observed, row_codes, shift_codes):
        rows, rank = left_factor.shape
        _, steps, cols, _ = observed.shape
        bf16, f32, i32 = jnp.bfloat16, jnp.float32, jnp.int32
        dma = pltpu.SemaphoreType.DMA
        vmem = pltpu.VMEM
        hbm = pl.BlockSpec(memory_space=pltpu.HBM)
        others = lanes // 2 - 1
        half = rows // 2
        shapes = (
            jax.ShapeDtypeStruct((rows, rank), bf16),
            jax.ShapeDtypeStruct((1, cols, rank), bf16),
        )
        results = pl.pallas_call(
            functools.partial(kernel, blocks, lanes),
            out_shape=shapes,
            in_specs=[hbm] * 5,
            out_specs=(hbm, hbm),
            scratch_shapes=[
                vmem((rows, rank), bf16),
                vmem((rows, rank), bf16),
                *[vmem((cols, rank), bf16)] * 7,
                vmem((steps - 1, cols, rows), bf16),
                vmem((cols, rows), bf16),
                vmem((1, rows), i32),
                vmem((1, rows), i32),
                vmem((1, steps, cols), i32),
                vmem((1, steps, cols), i32),
                vmem((steps, cols, WIDTH), i32),
                vmem((steps, cols, rows), bf16),
                vmem((rows, rank), f32),
                vmem((rows, rank), f32),
                *[vmem((half, rank), bf16)] * 7,
                vmem((others, half, rank), bf16),
                vmem((rows, rank), bf16),
                dma((4 + steps - 1,)),
                dma((CHUNKS,)), dma((CHUNKS,)),
                dma((2,)), dma((2,)),
                dma((SUBS,)), dma((SUBS,)),
                dma((others, SUBS)), dma((others, SUBS)),
                dma((1 + others, SUBS)), dma((1 + others, SUBS)),
                dma((CHUNKS,)), dma((CHUNKS,)),
                dma((CHUNKS,)), dma((CHUNKS,)),
                dma((1,)), dma((1,)),
                dma((PIECES,)), dma((PIECES,)),
                dma((PIECES,)), dma((PIECES,)),
                dma((others, PIECES)), dma((others, PIECES)),
                dma((PIECES,)), dma((PIECES,)),
                dma((3,)),
            ],
            compiler_params=pltpu.CompilerParams(
                collective_id=0, has_side_effects=True, vmem_limit_bytes=67043328
            ),
        )(
            left_factor, right_factor, observed,
            row_codes.reshape(1, rows), shift_codes,
        )
        return pl.pallas_call(
            place,
            out_shape=shapes,
            in_specs=[hbm] * 2,
            out_specs=(hbm, hbm),
            scratch_shapes=[pltpu.VMEM((2, max(rows, cols), rank), bf16), dma((2, PARTS)), dma((2, PARTS))],
            compiler_params=pltpu.CompilerParams(vmem_limit_bytes=67043328),
        )(*results)

    in_specs = (
        P("blk", None),
        P("lane", "blk", None),
        P("lane", None, None, "blk"),
        P("blk"),
        P("lane", None, "blk"),
    )
    out_specs = (P("blk", None), P("lane", "blk", None))
    return jax.shard_map(local, mesh=mesh, in_specs=in_specs, out_specs=out_specs, check_vma=False)
```

time: 56.5 us -> 59.6 us (1.055)
  the two profiles are of different devices: /device:TPU:0 before, /device:TPU:19 now
where the time goes in v1:
time: 59.6 us; the launch traced here: 59.4 us
  Pallas kernels  58.7 us (98%)
  between operations  0.64 us (1%)
    pallas_call x1, Pallas kernels, local(): pl.pallas_call(functools.partial(kernel, blocks, lanes), out_shape=shapes...  56.7 us
    pallas_call x1, Pallas kernels, local(): pl.pallas_call(place, out_shape=shapes, in_specs=[hbm] * 2, out_specs=(hb...  1.98 us

profile of v1, /device:TPU:19, one launch (start us, length us, event | category | flops | bytes accessed | tf_op | source)
XLA Modules:
  0.0 59.4 jit_solution(2860668036059558340)
XLA Ops:
  0.6 56.7 %shard_map.68 = (bf16[512,512]{1,0:T(8,128)(2,1)}, bf16[1,512,512]{2,1,0:T(8,128)(2,1)}) custom-call(bf16[512,512]{1,0:T(8,128)(2,1)} %left_hbm.1, bf16[1,512,512]{2,1,0:T(8,128)(2,1)} %right_hbm.1, bf16[1,4,512,512]{3,2,1,0:T(8,128)(2,1)} %obs_hbm.1, s32[1,512]{1,0:T(1,128)} %bitcast.1, s32[1,4,512]{2,1,0:T(4,128)} %shift_hbm.1), custom_call_target="tpu_custom_call" | custom-call | tf_op jit(solution)/shard_map/pallas_call | solution.py:378
  57.4 2.0 %shard_map.69 = (bf16[512,512]{1,0:T(8,128)(2,1)}, bf16[1,512,512]{2,1,0:T(8,128)(2,1)}) custom-call(bf16[512,512]{1,0:T(8,128)(2,1)} %get-tuple-element.4.left_from, bf16[1,512,512]{2,1,0:T(8,128)(2,1)} %get-tuple-element.5.right_from), custom_call_target="tpu_custom_call" | custom-call | tf_op jit(solution)/shard_map/pallas_call | solution.py:422

commit v2 on v1

--- a/solution.py
+++ b/solution.py
@@ -11,7 +11,10 @@
 step_right = 0.25
 step_left = 0.1
 
-CHUNKS = 4
+CHUNKS = 8
+LAG = 5
+HOLD = 4
+EARLY = 3
 WIDTH = 128
 PARTS = 2
 PIECES = 4
@@ -30,7 +33,7 @@
     load_sem, tile_send, tile_recv, table_send, table_recv, share_send, share_recv,
     peer_share_send, peer_share_recv, pair_share_send, pair_share_recv,
     hop_send, hop_recv, turn_send, turn_recv, back_send, back_recv, ret_send, ret_recv,
-    swap_send, swap_recv, cross_send, cross_recv, last_send, last_recv, out_sem,
+    swap_send, swap_recv, cross_send, cross_recv, last_send, last_recv, out_sem, clear_sem,
 ):
     steps, cols, rows = errs.shape
     rank = left.shape[1]
@@ -62,6 +65,8 @@
         pl.semaphore_signal(barrier, inc=1, device_id={"blk": target}, device_id_type=MESH)
     for friend in [pair] + peers:
         pl.semaphore_signal(barrier, inc=1, device_id={"lane": friend}, device_id_type=MESH)
+    pl.semaphore_signal(barrier, inc=1, device_id={"blk": ahead2, "lane": lane}, device_id_type=MESH)
+    pl.semaphore_signal(barrier, inc=1, device_id={"blk": ahead2, "lane": pair}, device_id_type=MESH)
 
     def remote(source, target, send, recv, **place):
         return pltpu.make_async_remote_copy(
@@ -151,7 +156,7 @@
 
     loads[0].wait()
     turn(0, shift)
-    pl.semaphore_wait(barrier, 3 + 1 + len(peers))
+    pl.semaphore_wait(barrier, 5 + 1 + len(peers))
     for u in range(SUBS):
         lend(u).start()
     for copy in tables:
@@ -180,6 +185,12 @@
             for u in range(SUBS):
                 lend_pair(m, u).wait_recv()
 
+    back = remote(back_out, back_in, back_send.at[0], back_recv.at[0], lane=pair)
+
+    def send_back():
+        back_out[...] = grad_g[pl.ds(other, half), :].astype(jnp.bfloat16)
+        back.start()
+
     @pl.when(odd == 0)
     def _():
         pl.loop(0, CHUNKS)(lambda k: tile(k, 0, first, inner))
@@ -189,21 +200,30 @@
         turn(3, shift)
         gather()
 
-        @pl.loop(0, CHUNKS)
-        def _(k):
+        def guest_visit(k):
             give(k).wait_recv()
-            tile(k, 1, inner, hop_out, guest=True)
+            tile(k, GUEST, inner, hop_out, guest=True)
             hop(k).start()
 
-        grad_g[...] = outer(errs[1], inner[...])
-        loads[5].wait()
-
-        @pl.loop(0, CHUNKS)
-        def _(k):
+        def home_visit(k):
             hop(k).wait_recv()
             tile(k, 2, hop_in, turn_out)
             cross_over(k).start()
 
+        loads[5].wait()
+        pl.loop(0, LAG)(guest_visit)
+        pl.loop(0, CHUNKS)(lambda k: give(k).wait_send())
+        pl.semaphore_signal(clear_sem, inc=1, device_id={"lane": pair}, device_id_type=MESH)
+        pl.semaphore_wait(clear_sem, 1)
+
+        @pl.loop(LAG, CHUNKS)
+        def _(k):
+            home_visit(k - LAG)
+            guest_visit(k)
+
+        grad_g[...] = outer(errs[GUEST], inner[...])
+        send_back()
+        pl.loop(CHUNKS - LAG, CHUNKS)(home_visit)
         grad[...] += outer(errs[2], hop_in[...])
 
     @pl.when(odd == 1)
@@ -220,24 +240,37 @@
         gather()
         loads[5].wait()
 
-        @pl.loop(0, CHUNKS)
-        def _(k):
+        def visits(k):
             give(k).wait_recv()
             hop(k).wait_recv()
-            tile(k, 1, hop_in, inner, guest=True)
+            tile(k, GUEST, hop_in, inner, guest=True)
             tile(k, 2, inner, turn_out)
+
+        pl.loop(0, HOLD)(visits)
+        pl.loop(0, CHUNKS - EARLY)(lambda k: give(k).wait_send())
+        for place_lane in (lane, pair):
+            pl.semaphore_signal(clear_sem, inc=1, device_id={"blk": behind2, "lane": place_lane}, device_id_type=MESH)
+        pl.semaphore_wait(clear_sem, 2)
+        pl.loop(0, HOLD)(lambda k: cross_over(k).start())
+
+        @pl.loop(HOLD, CHUNKS)
+        def _(k):
+            visits(k)
             cross_over(k).start()
 
-        grad_g[...] = outer(errs[1], hop_in[...])
+        grad_g[...] = outer(errs[GUEST], hop_in[...])
+        send_back()
         grad[...] += outer(errs[2], inner[...])
-
-    back = remote(back_out, back_in, back_send.at[0], back_recv.at[0], lane=pair)
-    back_out[...] = grad_g[pl.ds(other, half), :].astype(jnp.bfloat16)
-    back.start()
+        pl.loop(CHUNKS - EARLY, CHUNKS)(lambda k: give(k).wait_send())
 
     def give_back(q):
         span = pl.ds(q * part, part)
         return remote(ret_out.at[span], ret_in.at[span], ret_send.at[q], ret_recv.at[q], blk=partner)
+
+    back.wait_recv()
+    ret_out[...] = (grad_g[pl.ds(mine, half), :] + back_in[...].astype(jnp.float32)).astype(jnp.bfloat16)
+    for q in range(PIECES):
+        give_back(q).start()
 
     loads[6].wait()
     last = steps - 1
@@ -249,11 +282,6 @@
 
     early = (CHUNKS - 1) * size
     grad[...] += outer(errs[last, pl.ds(0, early)], turn_in[pl.ds(0, early)])
-    back.wait_recv()
-    ret_out[...] = (grad_g[pl.ds(mine, half), :] + back_in[...].astype(jnp.float32)).astype(jnp.bfloat16)
-    for q in range(PIECES):
-        give_back(q).start()
-
     tail = pl.ds(early, size)
     cross_over(CHUNKS - 1).wait_recv()
     errs[last, tail, :] = error_of(CHUNKS - 1, last, turn_in[tail, :], left, codes, obs.at[natural.index(last)])
@@ -309,7 +337,6 @@
 
     @pl.loop(0, CHUNKS)
     def _(k):
-        give(k).wait_send()
         hop(k).wait_send()
         cross_over(k).wait_send()
 
@@ -411,6 +438,7 @@
                 dma((others, PIECES)), dma((others, PIECES)),
                 dma((PIECES,)), dma((PIECES,)),
                 dma((3,)),
+                pltpu.SemaphoreType.REGULAR,
             ],
             compiler_params=pltpu.CompilerParams(
                 collective_id=0, has_side_effects=True, vmem_limit_bytes=67043328

time: 59.6 us -> 54.6 us (0.916)
  Pallas kernels: 58.7 us -> 53.8 us
    pallas_call x1, Pallas kernels: 56.7 us -> 51.8 us  [local(): pl.pallas_call(functools.partial(kernel, blocks, lanes), out_shape=shapes...]
where the time goes in v2:
time: 54.6 us; the launch traced here: 54.4 us
  Pallas kernels  53.8 us (99%)
  between operations  0.64 us (1%)
    pallas_call x1, Pallas kernels, local(): pl.pallas_call(functools.partial(kernel, blocks, lanes), out_shape=shapes...  51.8 us
    pallas_call x1, Pallas kernels, local(): pl.pallas_call(place, out_shape=shapes, in_specs=[hbm] * 2, out_specs=(hb...  1.98 us

profile of v2, /device:TPU:19, one launch (start us, length us, event | category | flops | bytes accessed | tf_op | source)
XLA Modules:
  0.0 54.4 jit_solution(18309142566781687633)
XLA Ops:
  0.6 51.8 %shard_map.68 = (bf16[512,512]{1,0:T(8,128)(2,1)}, bf16[1,512,512]{2,1,0:T(8,128)(2,1)}) custom-call(bf16[512,512]{1,0:T(8,128)(2,1)} %left_hbm.1, bf16[1,512,512]{2,1,0:T(8,128)(2,1)} %right_hbm.1, bf16[1,4,512,512]{3,2,1,0:T(8,128)(2,1)} %obs_hbm.1, s32[1,512]{1,0:T(1,128)} %bitcast.1, s32[1,4,512]{2,1,0:T(4,128)} %shift_hbm.1), custom_call_target="tpu_custom_call" | custom-call | tf_op jit(solution)/shard_map/pallas_call | solution.py:405
  52.4 2.0 %shard_map.69 = (bf16[512,512]{1,0:T(8,128)(2,1)}, bf16[1,512,512]{2,1,0:T(8,128)(2,1)}) custom-call(bf16[512,512]{1,0:T(8,128)(2,1)} %get-tuple-element.4.left_from, bf16[1,512,512]{2,1,0:T(8,128)(2,1)} %get-tuple-element.5.right_from), custom_call_target="tpu_custom_call" | custom-call | tf_op jit(solution)/shard_map/pallas_call | solution.py:450

commit v3 on v2

--- a/solution.py
+++ b/solution.py
@@ -14,7 +14,7 @@
 CHUNKS = 8
 LAG = 5
 HOLD = 4
-EARLY = 3
+EARLY = 2
 WIDTH = 128
 PARTS = 2
 PIECES = 4

time: 54.6 us -> 50.3 us (0.921)
  the two profiles are of different devices: /device:TPU:19 before, /device:TPU:0 now
where the time goes in v3:
time: 50.3 us; the launch traced here: 50.1 us
  Pallas kernels  49.4 us (98%)
  between operations  0.64 us (1%)
    pallas_call x1, Pallas kernels, local(): pl.pallas_call(functools.partial(kernel, blocks, lanes), out_shape=shapes...  47.4 us
    pallas_call x1, Pallas kernels, local(): pl.pallas_call(place, out_shape=shapes, in_specs=[hbm] * 2, out_specs=(hb...  1.98 us

profile of v3, /device:TPU:0, one launch (start us, length us, event | category | flops | bytes accessed | tf_op | source)
XLA Modules:
  0.0 50.1 jit_solution(3967909483666225999)
XLA Ops:
  0.6 47.4 %shard_map.68 = (bf16[512,512]{1,0:T(8,128)(2,1)}, bf16[1,512,512]{2,1,0:T(8,128)(2,1)}) custom-call(bf16[512,512]{1,0:T(8,128)(2,1)} %left_hbm.1, bf16[1,512,512]{2,1,0:T(8,128)(2,1)} %right_hbm.1, bf16[1,4,512,512]{3,2,1,0:T(8,128)(2,1)} %obs_hbm.1, s32[1,512]{1,0:T(1,128)} %bitcast.1, s32[1,4,512]{2,1,0:T(4,128)} %shift_hbm.1), custom_call_target="tpu_custom_call" | custom-call | tf_op jit(solution)/shard_map/pallas_call | solution.py:405
  48.1 2.0 %shard_map.69 = (bf16[512,512]{1,0:T(8,128)(2,1)}, bf16[1,512,512]{2,1,0:T(8,128)(2,1)}) custom-call(bf16[512,512]{1,0:T(8,128)(2,1)} %get-tuple-element.4.left_from, bf16[1,512,512]{2,1,0:T(8,128)(2,1)} %get-tuple-element.5.right_from), custom_call_target="tpu_custom_call" | custom-call | tf_op jit(solution)/shard_map/pallas_call | solution.py:450

commit v4 on v3

--- a/solution.py
+++ b/solution.py
@@ -16,26 +16,27 @@
 HOLD = 4
 EARLY = 2
 WIDTH = 128
-PARTS = 2
 PIECES = 4
 SUBS = 2
 GUEST = 1
+VMEM_BYTES = 67043328
 MESH = pl.DeviceIdType.MESH
 
 
 def kernel(
     blocks, lanes,
     left_hbm, right_hbm, obs_hbm, codes_hbm, shift_hbm,
-    left_out, right_out,
-    left, left_g, first, inner, hop_out, hop_in, turn_out, turn_in, final,
+    result, final_out,
+    left, left_g, first, inner, hop_out, hop_in, turn_out, turn_in,
     obs, obs_g, codes, codes_g, shift, shift_g, turned, errs,
-    grad, grad_g, back_out, back_in, ret_out, ret_in, pair_out, pair_in, peer_out, peer_in, result,
+    grad, grad_g, back_out, back_in, ret_out, ret_in, pair_out, pair_in, peer_out, peer_in,
     load_sem, tile_send, tile_recv, table_send, table_recv, share_send, share_recv,
     peer_share_send, peer_share_recv, pair_share_send, pair_share_recv,
     hop_send, hop_recv, turn_send, turn_recv, back_send, back_recv, ret_send, ret_recv,
-    swap_send, swap_recv, cross_send, cross_recv, last_send, last_recv, out_sem, clear_sem,
+    swap_send, swap_recv, cross_send, cross_recv, last_send, last_recv, clear_sem,
 ):
     steps, cols, rows = errs.shape
+    final = final_out.at[0]
     rank = left.shape[1]
     scale = 1.0 / math.sqrt(rank)
     size = cols // CHUNKS
@@ -320,12 +321,6 @@
 
     final[tail, :] = stepped(errs[last, tail, :], turn_in[tail, :], left)
 
-    outs = [
-        pltpu.make_async_copy(final, right_out.at[0], out_sem.at[0]),
-        pltpu.make_async_copy(result.at[pl.ds(mine, half)], left_out.at[pl.ds(mine, half)], out_sem.at[1]),
-        pltpu.make_async_copy(result.at[pl.ds(other, half)], left_out.at[pl.ds(other, half)], out_sem.at[2]),
-    ]
-    outs[0].start()
     for u in range(SUBS):
         lend(u).wait_send()
         for m in range(others):
@@ -351,38 +346,25 @@
             total = total + peer_in[m, span, :].astype(jnp.float32)
         result[here, :] = (left[here, :].astype(jnp.float32) - step_left * scale * total).astype(jnp.bfloat16)
         share(q).start()
-    outs[1].start()
     for q in range(PIECES):
         share(q).wait_recv()
-    outs[2].start()
     for q in range(PIECES):
         give_back(q).wait_send()
         swap(q).wait_send()
         for m in range(len(peers)):
             cross(m, q).wait_send()
         share(q).wait_send()
-    for copy in outs:
-        copy.wait()
-
-
-def place(left_from, right_from, left_to, right_to, held, in_sem, out_sem):
-    pairs = [(left_from, left_to), (right_from.at[0], right_to.at[0])]
-    rows = left_from.shape[0] // PARTS
-    moves = []
-    for which, (source, target) in enumerate(pairs):
-        for p in range(PARTS):
-            span = pl.ds(p * rows, rows)
-            moves.append((
-                pltpu.make_async_copy(source.at[span], held.at[which, span], in_sem.at[which, p]),
-                pltpu.make_async_copy(held.at[which, span], target.at[span], out_sem.at[which, p]),
-            ))
-    for inward, _ in moves:
-        inward.start()
-    for inward, outward in moves:
-        inward.wait()
-        outward.start()
-    for _, outward in moves:
-        outward.wait()
+
+
+def place(left_from, right_from, left_to, right_to, sem):
+    moves = [
+        pltpu.make_async_copy(left_from, left_to, sem.at[0]),
+        pltpu.make_async_copy(right_from, right_to, sem.at[1]),
+    ]
+    for move in moves:
+        move.start()
+    for move in moves:
+        move.wait()
 
 
 def solution(mesh):
@@ -396,6 +378,8 @@
         dma = pltpu.SemaphoreType.DMA
         vmem = pltpu.VMEM
         hbm = pl.BlockSpec(memory_space=pltpu.HBM)
+        here = pl.BlockSpec(memory_space=pltpu.VMEM)
+        room = VMEM_BYTES - 2 * (rows + cols) * rank
         others = lanes // 2 - 1
         half = rows // 2
         shapes = (
@@ -404,13 +388,13 @@
         )
         results = pl.pallas_call(
             functools.partial(kernel, blocks, lanes),
-            out_shape=shapes,
+            out_shape=(vmem((rows, rank), bf16), vmem((1, cols, rank), bf16)),
             in_specs=[hbm] * 5,
-            out_specs=(hbm, hbm),
+            out_specs=(here, here),
             scratch_shapes=[
                 vmem((rows, rank), bf16),
                 vmem((rows, rank), bf16),
-                *[vmem((cols, rank), bf16)] * 7,
+                *[vmem((cols, rank), bf16)] * 6,
                 vmem((steps - 1, cols, rows), bf16),
                 vmem((cols, rows), bf16),
                 vmem((1, rows), i32),
@@ -423,7 +407,6 @@
                 vmem((rows, rank), f32),
                 *[vmem((half, rank), bf16)] * 7,
                 vmem((others, half, rank), bf16),
-                vmem((rows, rank), bf16),
                 dma((4 + steps - 1,)),
                 dma((CHUNKS,)), dma((CHUNKS,)),
                 dma((2,)), dma((2,)),
@@ -437,11 +420,10 @@
                 dma((PIECES,)), dma((PIECES,)),
                 dma((others, PIECES)), dma((others, PIECES)),
                 dma((PIECES,)), dma((PIECES,)),
-                dma((3,)),
                 pltpu.SemaphoreType.REGULAR,
             ],
             compiler_params=pltpu.CompilerParams(
-                collective_id=0, has_side_effects=True, vmem_limit_bytes=67043328
+                collective_id=0, has_side_effects=True, vmem_limit_bytes=room
             ),
         )(
             left_factor, right_factor, observed,
@@ -450,11 +432,11 @@
         return pl.pallas_call(
             place,
             out_shape=shapes,
-            in_specs=[hbm] * 2,
+            in_specs=[here] * 2,
             out_specs=(hbm, hbm),
-            scratch_shapes=[pltpu.VMEM((2, max(rows, cols), rank), bf16), dma((2, PARTS)), dma((2, PARTS))],
-            compiler_params=pltpu.CompilerParams(vmem_limit_bytes=67043328),
-        )(*results)
+            scratch_shapes=[dma((2,))],
+            compiler_params=pltpu.CompilerParams(vmem_limit_bytes=room),
+        )(*[pltpu.with_memory_space_constraint(value, pltpu.VMEM) for value in results])
 
     in_specs = (
         P("blk", None),

time: 50.3 us -> 48.7 us (0.968)
  Pallas kernels: 49.4 us -> 47.8 us
    pallas_call x2, Pallas kernels: 49.4 us -> 47.8 us  [the longest x1 46.9 us: local(): pl.pallas_call(functools.partial(kernel, blocks, lanes), out_shape=(vmem(...]
where the time goes in v4:
time: 48.7 us; the launch traced here: 48.5 us
  Pallas kernels  47.8 us (98%)
  between operations  0.64 us (1%)
    pallas_call x1, Pallas kernels, local(): pl.pallas_call(functools.partial(kernel, blocks, lanes), out_shape=(vmem(...  46.9 us
    pallas_call x1, Pallas kernels, local(): pl.pallas_call(place, out_shape=shapes, in_specs=[here] * 2, out_specs=(h...  0.99 us

profile of v4, /device:TPU:0, one launch (start us, length us, event | category | flops | bytes accessed | tf_op | source)
XLA Modules:
  0.0 48.5 jit_solution(6155334859968867793)
XLA Ops:
  0.6 46.9 %shard_map.68 = (bf16[512,512]{1,0:T(8,128)(2,1)S(1)}, bf16[1,512,512]{2,1,0:T(8,128)(2,1)S(1)}) custom-call(bf16[512,512]{1,0:T(8,128)(2,1)} %left_hbm.1, bf16[1,512,512]{2,1,0:T(8,128)(2,1)} %right_hbm.1, bf16[1,4,512,512]{3,2,1,0:T(8,128)(2,1)} %obs_hbm.1, s32[1,512]{1,0:T(1,128)} %bitcast.1, s32[1,4,512]{2,1,0:T(4,128)} %shift_hbm.1), custom_call_target="tpu_custom_call" | custom-call | tf_op jit(solution)/shard_map/pallas_call | solution.py:389
  47.5 1.0 %shard_map.69 = (bf16[512,512]{1,0:T(8,128)(2,1)}, bf16[1,512,512]{2,1,0:T(8,128)(2,1)}) custom-call(bf16[512,512]{1,0:T(8,128)(2,1)S(1)} %get-tuple-element.4.left_from, bf16[1,512,512]{2,1,0:T(8,128)(2,1)S(1)} %get-tuple-element.5.right_from), custom_call_target="tpu_custom_call" | custom-call | tf_op jit(solution)/shard_map/pallas_call | solution.py:432

commit v5 on v4

--- a/solution.py
+++ b/solution.py
@@ -16,7 +16,7 @@
 HOLD = 4
 EARLY = 2
 WIDTH = 128
-PIECES = 4
+PIECES = 8
 SUBS = 2
 GUEST = 1
 VMEM_BYTES = 67043328
@@ -33,7 +33,7 @@
     load_sem, tile_send, tile_recv, table_send, table_recv, share_send, share_recv,
     peer_share_send, peer_share_recv, pair_share_send, pair_share_recv,
     hop_send, hop_recv, turn_send, turn_recv, back_send, back_recv, ret_send, ret_recv,
-    swap_send, swap_recv, cross_send, cross_recv, last_send, last_recv, clear_sem,
+    swap_send, swap_recv, cross_send, cross_recv, last_send, last_recv, clear_sem, go_sem,
 ):
     steps, cols, rows = errs.shape
     final = final_out.at[0]
@@ -66,8 +66,6 @@
         pl.semaphore_signal(barrier, inc=1, device_id={"blk": target}, device_id_type=MESH)
     for friend in [pair] + peers:
         pl.semaphore_signal(barrier, inc=1, device_id={"lane": friend}, device_id_type=MESH)
-    pl.semaphore_signal(barrier, inc=1, device_id={"blk": ahead2, "lane": lane}, device_id_type=MESH)
-    pl.semaphore_signal(barrier, inc=1, device_id={"blk": ahead2, "lane": pair}, device_id_type=MESH)
 
     def remote(source, target, send, recv, **place):
         return pltpu.make_async_remote_copy(
@@ -157,7 +155,7 @@
 
     loads[0].wait()
     turn(0, shift)
-    pl.semaphore_wait(barrier, 5 + 1 + len(peers))
+    pl.semaphore_wait(barrier, 3 + 1 + len(peers))
     for u in range(SUBS):
         lend(u).start()
     for copy in tables:
@@ -249,9 +247,10 @@
 
         pl.loop(0, HOLD)(visits)
         pl.loop(0, CHUNKS - EARLY)(lambda k: give(k).wait_send())
-        for place_lane in (lane, pair):
-            pl.semaphore_signal(clear_sem, inc=1, device_id={"blk": behind2, "lane": place_lane}, device_id_type=MESH)
-        pl.semaphore_wait(clear_sem, 2)
+        pl.semaphore_signal(clear_sem, inc=1, device_id={"lane": pair}, device_id_type=MESH)
+        pl.semaphore_wait(clear_sem, 1)
+        pl.semaphore_signal(go_sem, inc=1, device_id={"blk": behind2}, device_id_type=MESH)
+        pl.semaphore_wait(go_sem, 1)
         pl.loop(0, HOLD)(lambda k: cross_over(k).start())
 
         @pl.loop(HOLD, CHUNKS)
@@ -288,7 +287,7 @@
     errs[last, tail, :] = error_of(CHUNKS - 1, last, turn_in[tail, :], left, codes, obs.at[natural.index(last)])
 
     def finish(start):
-        span = pl.ds(start, half)
+        span = pl.ds(pl.multiple_of(start, width), width)
         return grad[span, :] + outer(errs[last, tail, span], turn_in[tail, :])
 
     def swap(q):
@@ -303,10 +302,12 @@
         span = pl.ds(pl.multiple_of(mine + q * part, part), part)
         return remote(result.at[span], result.at[span], last_send.at[q], last_recv.at[q], lane=pair)
 
-    pair_out[...] = finish(other).astype(jnp.bfloat16)
-    for q in range(PIECES):
-        swap(q).start()
-    grad[pl.ds(mine, half), :] = finish(mine)
+    for start in range(0, half, width):
+        pair_out[pl.ds(start, width), :] = finish(other + start).astype(jnp.bfloat16)
+        for q in range(start // part, (start + width) // part):
+            swap(q).start()
+    for start in range(0, half, width):
+        grad[pl.ds(pl.multiple_of(mine + start, width), width), :] = finish(mine + start)
     for q in range(PIECES):
         span = pl.ds(q * part, part)
         swap(q).wait_recv()
@@ -421,6 +422,7 @@
                 dma((others, PIECES)), dma((others, PIECES)),
                 dma((PIECES,)), dma((PIECES,)),
                 pltpu.SemaphoreType.REGULAR,
+                pltpu.SemaphoreType.REGULAR,
             ],
             compiler_params=pltpu.CompilerParams(
                 collective_id=0, has_side_effects=True, vmem_limit_bytes=room

time: 48.7 us -> 46.8 us (0.961)
  Pallas kernels: 47.8 us -> 46 us
    pallas_call x1, Pallas kernels: 46.9 us -> 45 us  [local(): pl.pallas_call(functools.partial(kernel, blocks, lanes), out_shape=(vmem(...]
where the time goes in v5:
time: 46.8 us; the launch traced here: 46.6 us
  Pallas kernels  46 us (98%)
  between operations  0.64 us (1%)
    pallas_call x1, Pallas kernels, local(): pl.pallas_call(functools.partial(kernel, blocks, lanes), out_shape=(vmem(...  45 us
    pallas_call x1, Pallas kernels, local(): pl.pallas_call(place, out_shape=shapes, in_specs=[here] * 2, out_specs=(h...  0.99 us

profile of v5, /device:TPU:0, one launch (start us, length us, event | category | flops | bytes accessed | tf_op | source)
XLA Modules:
  0.0 46.6 jit_solution(17778922778947097656)
XLA Ops:
  0.6 45.0 %shard_map.68 = (bf16[512,512]{1,0:T(8,128)(2,1)S(1)}, bf16[1,512,512]{2,1,0:T(8,128)(2,1)S(1)}) custom-call(bf16[512,512]{1,0:T(8,128)(2,1)} %left_hbm.1, bf16[1,512,512]{2,1,0:T(8,128)(2,1)} %right_hbm.1, bf16[1,4,512,512]{3,2,1,0:T(8,128)(2,1)} %obs_hbm.1, s32[1,512]{1,0:T(1,128)} %bitcast.1, s32[1,4,512]{2,1,0:T(4,128)} %shift_hbm.1), custom_call_target="tpu_custom_call" | custom-call | tf_op jit(solution)/shard_map/pallas_call | solution.py:390
  45.6 1.0 %shard_map.69 = (bf16[512,512]{1,0:T(8,128)(2,1)}, bf16[1,512,512]{2,1,0:T(8,128)(2,1)}) custom-call(bf16[512,512]{1,0:T(8,128)(2,1)S(1)} %get-tuple-element.4.left_from, bf16[1,512,512]{2,1,0:T(8,128)(2,1)S(1)} %get-tuple-element.5.right_from), custom_call_target="tpu_custom_call" | custom-call | tf_op jit(solution)/shard_map/pallas_call | solution.py:434

commit v6 on v5

--- a/solution.py
+++ b/solution.py
@@ -13,8 +13,9 @@
 
 CHUNKS = 8
 LAG = 5
-HOLD = 4
+HOLD = 1
 EARLY = 2
+RETURN = 5
 WIDTH = 128
 PIECES = 8
 SUBS = 2
@@ -29,23 +30,25 @@
     result, final_out,
     left, left_g, first, inner, hop_out, hop_in, turn_out, turn_in,
     obs, obs_g, codes, codes_g, shift, shift_g, turned, errs,
-    grad, grad_g, back_out, back_in, ret_out, ret_in, pair_out, pair_in, peer_out, peer_in,
+    grad, grad_g, back_out, back_in, ret_sum, ret_part, ret_out, ret_in, pair_out, pair_in, peer_out, peer_in,
     load_sem, tile_send, tile_recv, table_send, table_recv, share_send, share_recv,
     peer_share_send, peer_share_recv, pair_share_send, pair_share_recv,
-    hop_send, hop_recv, turn_send, turn_recv, back_send, back_recv, ret_send, ret_recv,
-    swap_send, swap_recv, cross_send, cross_recv, last_send, last_recv, clear_sem, go_sem,
+    hop_send, hop_recv, turn_send, turn_recv, back_send, back_recv, fold_send, fold_recv, ret_send, ret_recv,
+    swap_send, swap_recv, cross_send, cross_recv, last_send, last_recv, clear_sem, go_sem, ready_sem,
 ):
     steps, cols, rows = errs.shape
     final = final_out.at[0]
     rank = left.shape[1]
     scale = 1.0 / math.sqrt(rank)
     size = cols // CHUNKS
+    ready = cols - EARLY * size
     half = rows // 2
     part = half // PIECES
     own = rows // lanes
     sub = own // SUBS
     width = turned.shape[2]
     others = lanes // 2 - 1
+    quota = own // part
     blk = lax.axis_index("blk")
     lane = lax.axis_index("lane")
     odd = lax.rem(blk, 2)
@@ -55,6 +58,7 @@
     ahead2 = lax.rem(blk + 2, blocks)
     behind2 = lax.rem(blk + blocks - 2, blocks)
     side = lax.rem(lane, 2)
+    chip = lane // 2
     pair = lane + 1 - 2 * side
     peers = [lax.rem(lane + 2 * hop, lanes) for hop in range(1, lanes // 2)]
     sources = [lax.rem(lane + lanes - 2 * hop, lanes) for hop in range(1, lanes // 2)]
@@ -62,10 +66,30 @@
     other = pl.multiple_of((1 - side) * half, half)
 
     barrier = pltpu.get_barrier_semaphore()
-    for target in (partner, behind, behind2):
-        pl.semaphore_signal(barrier, inc=1, device_id={"blk": target}, device_id_type=MESH)
-    for friend in [pair] + peers:
-        pl.semaphore_signal(barrier, inc=1, device_id={"lane": friend}, device_id_type=MESH)
+
+    def greet(**place):
+        pl.semaphore_signal(barrier, inc=1, device_id=place, device_id_type=MESH)
+
+    def answer(which, **place):
+        pl.semaphore_signal(ready_sem.at[which], inc=1, device_id=place, device_id_type=MESH)
+
+    def await_answer(which):
+        pl.semaphore_wait(ready_sem.at[which], 1)
+
+    inner_blk = blk >= 2
+    wraps = blk >= blocks - 2
+    ends = blk == blocks - 1
+    greet(lane=pair)
+    pl.when(odd == 0)(lambda: greet(blk=partner))
+    pl.when((odd == 1) & ~ends)(lambda: greet(blk=ahead))
+    pl.when(~wraps)(lambda: greet(blk=ahead2))
+    pl.when(~inner_blk)(lambda: greet(blk=behind2))
+    pl.when(blk == 0)(lambda: greet(blk=behind))
+    greeters = 1 + odd + ((odd == 0) & inner_blk).astype(jnp.int32) + inner_blk.astype(jnp.int32)
+    greeters += wraps.astype(jnp.int32) + ends.astype(jnp.int32)
+    for peer in peers:
+        pl.when(peer > lane)(functools.partial(greet, lane=peer))
+        greeters += (peer < lane).astype(jnp.int32)
 
     def remote(source, target, send, recv, **place):
         return pltpu.make_async_remote_copy(
@@ -93,19 +117,29 @@
 
     def lend(u):
         span = piece(lane, u)
-        return remote(left_hbm.at[span], left_g.at[span], share_send.at[u], share_recv.at[u], blk=partner)
+        return remote(left_hbm.at[span], left_g.at[span], share_send.at[0], share_recv.at[u], blk=partner)
 
     def lend_peer(m, u):
         span = piece(lane, u)
-        return remote(left_g.at[span], left_g.at[span], peer_share_send.at[m, u], peer_share_recv.at[m, u], lane=peers[m])
+        return remote(left_g.at[span], left_g.at[span], peer_share_send.at[m], peer_share_recv.at[m, u], lane=peers[m])
 
     def lend_pair(m, u):
         span = piece(lane if m == 0 else sources[m - 1], u)
-        return remote(left_g.at[span], left_g.at[span], pair_share_send.at[m, u], pair_share_recv.at[m, u], lane=pair)
+        return remote(left_g.at[span], left_g.at[span], pair_share_send.at[m], pair_share_recv.at[m, u], lane=pair)
+
+    def given(k):
+        span = chunk(k)
+        return remote(obs_hbm.at[0, GUEST, span], obs_g.at[span], tile_send.at[0], tile_recv.at[k], blk=partner)
+
+    def give_sent(late):
+        span = pl.ds(ready, cols - ready) if late else pl.ds(0, ready)
+        return remote(obs_hbm.at[0, GUEST, span], obs_g.at[span], tile_send.at[late], tile_recv.at[0], blk=partner)
 
     def give(k):
         span = chunk(k)
-        return remote(obs_hbm.at[0, GUEST, span], obs_g.at[span], tile_send.at[k], tile_recv.at[k], blk=partner)
+        return remote(
+            obs_hbm.at[0, GUEST, span], obs_g.at[span], tile_send.at[int(k >= CHUNKS - EARLY)], tile_recv.at[k], blk=partner
+        )
 
     tables = [
         remote(codes_hbm, codes_g, table_send.at[0], table_recv.at[0], blk=partner),
@@ -114,11 +148,11 @@
 
     def hop(k):
         span = chunk(k)
-        return remote(hop_out.at[span], hop_in.at[span], hop_send.at[k], hop_recv.at[k], blk=ahead2)
+        return remote(hop_out.at[span], hop_in.at[span], hop_send.at[0], hop_recv.at[k], blk=ahead2)
 
     def cross_over(k):
         span = chunk(k)
-        return remote(turn_out.at[span], turn_in.at[span], turn_send.at[k], turn_recv.at[k], blk=ahead)
+        return remote(turn_out.at[span], turn_in.at[span], turn_send.at[0], turn_recv.at[k], blk=ahead)
 
     def turn(s, table):
         for start in range(0, cols, width):
@@ -150,12 +184,24 @@
         errs[s, span, :] = error
         target[span, :] = stepped(error, block, factor)
 
+    last = steps - 1
+
+    def last_visit(k):
+        cross_over(k).wait_recv()
+        tile(k, last, turn_in, final)
+
     def outer(error, block):
         return lax.dot_general(error, block, (((0,), (0,)), ((), ())), preferred_element_type=jnp.float32)
 
     loads[0].wait()
     turn(0, shift)
-    pl.semaphore_wait(barrier, 3 + 1 + len(peers))
+    pl.semaphore_wait(barrier, greeters)
+    pl.when(odd == 1)(lambda: answer(0, blk=partner))
+    pl.when((odd == 0) & inner_blk)(lambda: answer(1, blk=behind))
+    pl.when(inner_blk)(lambda: answer(2, blk=behind2))
+    for m, peer in enumerate(peers):
+        pl.when(peer < lane)(functools.partial(answer, 3 + others - 1 - m, lane=peer))
+    pl.when(odd == 0)(lambda: await_answer(0))
     for u in range(SUBS):
         lend(u).start()
     for copy in tables:
@@ -166,6 +212,8 @@
         copy.wait()
 
     def relay():
+        for m, peer in enumerate(peers):
+            pl.when(peer > lane)(functools.partial(await_answer, 3 + m))
         for u in range(SUBS):
             lend(u).wait_recv()
             for m in range(others):
@@ -190,6 +238,29 @@
         back_out[...] = grad_g[pl.ds(other, half), :].astype(jnp.bfloat16)
         back.start()
 
+    def fold(m):
+        span = pl.ds(pl.multiple_of((peers[m] // 2) * own, own), own)
+        return remote(ret_sum.at[span], ret_part.at[m], fold_send.at[m], fold_recv.at[m], lane=peers[m])
+
+    def give_back(q):
+        span = pl.ds(q * part, part)
+        return remote(ret_out.at[span], ret_in.at[span], ret_send.at[0], ret_recv.at[q], blk=partner)
+
+    def send_fold():
+        back.wait_recv()
+        ret_sum[...] = (grad_g[pl.ds(mine, half), :] + back_in[...].astype(jnp.float32)).astype(jnp.bfloat16)
+        for m in range(others):
+            fold(m).start()
+
+    def send_return():
+        total = ret_sum[pl.ds(pl.multiple_of(chip * own, own), own), :].astype(jnp.float32)
+        for m in range(others):
+            fold(m).wait_recv()
+            total = total + ret_part[m].astype(jnp.float32)
+        ret_out[...] = total.astype(jnp.bfloat16)
+        for q in range(quota):
+            give_back(q).start()
+
     @pl.when(odd == 0)
     def _():
         pl.loop(0, CHUNKS)(lambda k: tile(k, 0, first, inner))
@@ -199,8 +270,10 @@
         turn(3, shift)
         gather()
 
+        pl.when(~wraps)(lambda: await_answer(2))
+
         def guest_visit(k):
-            give(k).wait_recv()
+            given(k).wait_recv()
             tile(k, GUEST, inner, hop_out, guest=True)
             hop(k).start()
 
@@ -210,8 +283,10 @@
             cross_over(k).start()
 
         loads[5].wait()
+        loads[6].wait()
         pl.loop(0, LAG)(guest_visit)
-        pl.loop(0, CHUNKS)(lambda k: give(k).wait_send())
+        give_sent(0).wait_send()
+        give_sent(1).wait_send()
         pl.semaphore_signal(clear_sem, inc=1, device_id={"lane": pair}, device_id_type=MESH)
         pl.semaphore_wait(clear_sem, 1)
 
@@ -222,12 +297,23 @@
 
         grad_g[...] = outer(errs[GUEST], inner[...])
         send_back()
-        pl.loop(CHUNKS - LAG, CHUNKS)(home_visit)
+        pl.loop(CHUNKS - LAG, CHUNKS - LAG + 2)(home_visit)
+        send_fold()
+
+        @pl.loop(CHUNKS - LAG + 2, CHUNKS)
+        def _(k):
+            home_visit(k)
+            last_visit(k - (CHUNKS - LAG + 2))
+
         grad[...] += outer(errs[2], hop_in[...])
 
     @pl.when(odd == 1)
     def _():
-        @pl.loop(0, CHUNKS)
+        tile(0, 0, first, hop_out)
+        pl.when(~wraps)(lambda: await_answer(2))
+        hop(0).start()
+
+        @pl.loop(1, CHUNKS)
         def _(k):
             tile(k, 0, first, hop_out)
             hop(k).start()
@@ -238,19 +324,21 @@
         turn(3, shift)
         gather()
         loads[5].wait()
+        loads[6].wait()
 
         def visits(k):
-            give(k).wait_recv()
+            given(k).wait_recv()
             hop(k).wait_recv()
             tile(k, GUEST, hop_in, inner, guest=True)
             tile(k, 2, inner, turn_out)
 
         pl.loop(0, HOLD)(visits)
-        pl.loop(0, CHUNKS - EARLY)(lambda k: give(k).wait_send())
+        give_sent(0).wait_send()
         pl.semaphore_signal(clear_sem, inc=1, device_id={"lane": pair}, device_id_type=MESH)
         pl.semaphore_wait(clear_sem, 1)
         pl.semaphore_signal(go_sem, inc=1, device_id={"blk": behind2}, device_id_type=MESH)
         pl.semaphore_wait(go_sem, 1)
+        pl.when(~ends)(lambda: await_answer(1))
         pl.loop(0, HOLD)(lambda k: cross_over(k).start())
 
         @pl.loop(HOLD, CHUNKS)
@@ -261,24 +349,12 @@
         grad_g[...] = outer(errs[GUEST], hop_in[...])
         send_back()
         grad[...] += outer(errs[2], inner[...])
-        pl.loop(CHUNKS - EARLY, CHUNKS)(lambda k: give(k).wait_send())
-
-    def give_back(q):
-        span = pl.ds(q * part, part)
-        return remote(ret_out.at[span], ret_in.at[span], ret_send.at[q], ret_recv.at[q], blk=partner)
-
-    back.wait_recv()
-    ret_out[...] = (grad_g[pl.ds(mine, half), :] + back_in[...].astype(jnp.float32)).astype(jnp.bfloat16)
-    for q in range(PIECES):
-        give_back(q).start()
-
-    loads[6].wait()
-    last = steps - 1
-
-    @pl.loop(0, CHUNKS - 1)
-    def _(k):
-        cross_over(k).wait_recv()
-        tile(k, last, turn_in, final)
+        give_sent(1).wait_send()
+        send_fold()
+
+    pl.loop(lax.select(odd == 0, LAG - 2, 0), RETURN)(last_visit)
+    send_return()
+    pl.loop(RETURN, CHUNKS - 1)(last_visit)
 
     early = (CHUNKS - 1) * size
     grad[...] += outer(errs[last, pl.ds(0, early)], turn_in[pl.ds(0, early)])
@@ -291,16 +367,16 @@
         return grad[span, :] + outer(errs[last, tail, span], turn_in[tail, :])
 
     def swap(q):
-        span = pl.ds(q * part, part)
-        return remote(pair_out.at[span], pair_in.at[span], swap_send.at[q], swap_recv.at[q], lane=pair)
-
-    def cross(m, q):
-        span = pl.ds(q * part, part)
-        return remote(peer_out.at[span], peer_in.at[m, span], cross_send.at[m, q], cross_recv.at[m, q], lane=peers[m])
-
-    def share(q):
-        span = pl.ds(pl.multiple_of(mine + q * part, part), part)
-        return remote(result.at[span], result.at[span], last_send.at[q], last_recv.at[q], lane=pair)
+        span = pl.ds(pl.multiple_of(q * part, part), part)
+        return remote(pair_out.at[span], pair_in.at[span], swap_send.at[0], swap_recv.at[q], lane=pair)
+
+    def cross(m, n):
+        span = pl.ds(pl.multiple_of(n * part, part), part)
+        return remote(peer_out.at[span], peer_in.at[m, span], cross_send.at[m], cross_recv.at[m, n], lane=peers[m])
+
+    def share(n):
+        span = pl.ds(pl.multiple_of(mine + n * part, part), part)
+        return remote(result.at[span], result.at[span], last_send.at[0], last_recv.at[0], lane=pair)
 
     for start in range(0, half, width):
         pair_out[pl.ds(start, width), :] = finish(other + start).astype(jnp.bfloat16)
@@ -309,52 +385,54 @@
     for start in range(0, half, width):
         grad[pl.ds(pl.multiple_of(mine + start, width), width), :] = finish(mine + start)
     for q in range(PIECES):
-        span = pl.ds(q * part, part)
-        swap(q).wait_recv()
-        give_back(q).wait_recv()
-        peer_out[span, :] = (
-            grad[pl.ds(pl.multiple_of(mine + q * part, part), part), :]
+        n = lax.rem((chip + 1) * quota + q, PIECES)
+        span = pl.ds(pl.multiple_of(n * part, part), part)
+        swap(n).wait_recv()
+        total = (
+            grad[pl.ds(pl.multiple_of(mine + n * part, part), part), :]
             + pair_in[span, :].astype(jnp.float32)
-            + ret_in[span, :].astype(jnp.float32)
-        ).astype(jnp.bfloat16)
+        )
+        if q >= PIECES - quota:
+            r = q - (PIECES - quota)
+            give_back(r).wait_recv()
+            total = total + ret_in[pl.ds(r * part, part), :].astype(jnp.float32)
+        peer_out[span, :] = total.astype(jnp.bfloat16)
         for m in range(len(peers)):
-            cross(m, q).start()
+            cross(m, n).start()
 
     final[tail, :] = stepped(errs[last, tail, :], turn_in[tail, :], left)
 
-    for u in range(SUBS):
-        lend(u).wait_send()
-        for m in range(others):
-            lend_peer(m, u).wait_send()
-        for m in range(1 + others):
-            lend_pair(m, u).wait_send()
+    lent = pl.ds(pl.multiple_of(lane * own, own), own)
+    remote(left_hbm.at[lent], left_g.at[lent], share_send.at[0], share_recv.at[0], blk=partner).wait_send()
+    for m in range(others):
+        remote(left_g.at[lent], left_g.at[lent], peer_share_send.at[m], peer_share_recv.at[m, 0], lane=peers[m]).wait_send()
+    for m in range(1 + others):
+        remote(left_g.at[lent], left_g.at[lent], pair_share_send.at[m], pair_share_recv.at[m, 0], lane=pair).wait_send()
     for copy in tables:
         copy.wait_send()
-
-    @pl.loop(0, CHUNKS)
-    def _(k):
-        hop(k).wait_send()
-        cross_over(k).wait_send()
-
+    remote(hop_out, hop_in, hop_send.at[0], hop_recv.at[0], blk=ahead2).wait_send()
+    remote(turn_out, turn_in, turn_send.at[0], turn_recv.at[0], blk=ahead).wait_send()
     back.wait_send()
+    for m in range(others):
+        fold(m).wait_send()
 
     for q in range(PIECES):
-        span = pl.ds(q * part, part)
-        here = pl.ds(pl.multiple_of(mine + q * part, part), part)
+        n = lax.rem(chip * quota + q, PIECES)
+        span = pl.ds(pl.multiple_of(n * part, part), part)
+        here = pl.ds(pl.multiple_of(mine + n * part, part), part)
         total = peer_out[span, :].astype(jnp.float32)
         for m in range(len(peers)):
-            cross(m, q).wait_recv()
+            cross(m, n).wait_recv()
             total = total + peer_in[m, span, :].astype(jnp.float32)
         result[here, :] = (left[here, :].astype(jnp.float32) - step_left * scale * total).astype(jnp.bfloat16)
-        share(q).start()
-    for q in range(PIECES):
-        share(q).wait_recv()
-    for q in range(PIECES):
-        give_back(q).wait_send()
-        swap(q).wait_send()
-        for m in range(len(peers)):
-            cross(m, q).wait_send()
-        share(q).wait_send()
+        share(n).start()
+    shared = result.at[pl.ds(mine, half)]
+    remote(shared, shared, last_send.at[0], last_recv.at[0], lane=pair).wait_recv()
+    remote(ret_out, ret_in, ret_send.at[0], ret_recv.at[0], blk=partner).wait_send()
+    remote(pair_out, pair_in, swap_send.at[0], swap_recv.at[0], lane=pair).wait_send()
+    for m in range(len(peers)):
+        remote(peer_out, peer_in.at[m], cross_send.at[m], cross_recv.at[m, 0], lane=peers[m]).wait_send()
+    remote(shared, shared, last_send.at[0], last_recv.at[0], lane=pair).wait_send()
 
 
 def place(left_from, right_from, left_to, right_to, sem):
@@ -406,23 +484,28 @@
                 vmem((steps, cols, rows), bf16),
                 vmem((rows, rank), f32),
                 vmem((rows, rank), f32),
-                *[vmem((half, rank), bf16)] * 7,
+                *[vmem((half, rank), bf16)] * 3,
+                vmem((others, rows // lanes, rank), bf16),
+                *[vmem((rows // lanes, rank), bf16)] * 2,
+                *[vmem((half, rank), bf16)] * 3,
                 vmem((others, half, rank), bf16),
                 dma((4 + steps - 1,)),
-                dma((CHUNKS,)), dma((CHUNKS,)),
+                dma((2,)), dma((CHUNKS,)),
                 dma((2,)), dma((2,)),
-                dma((SUBS,)), dma((SUBS,)),
-                dma((others, SUBS)), dma((others, SUBS)),
-                dma((1 + others, SUBS)), dma((1 + others, SUBS)),
-                dma((CHUNKS,)), dma((CHUNKS,)),
-                dma((CHUNKS,)), dma((CHUNKS,)),
+                dma((1,)), dma((SUBS,)),
+                dma((others,)), dma((others, SUBS)),
+                dma((1 + others,)), dma((1 + others, SUBS)),
+                dma((1,)), dma((CHUNKS,)),
+                dma((1,)), dma((CHUNKS,)),
                 dma((1,)), dma((1,)),
-                dma((PIECES,)), dma((PIECES,)),
-                dma((PIECES,)), dma((PIECES,)),
-                dma((others, PIECES)), dma((others, PIECES)),
-                dma((PIECES,)), dma((PIECES,)),
+                dma((others,)), dma((others,)),
+                dma((1,)), dma((PIECES,)),
+                dma((1,)), dma((PIECES,)),
+                dma((others,)), dma((others, PIECES)),
+                dma((1,)), dma((1,)),
                 pltpu.SemaphoreType.REGULAR,
                 pltpu.SemaphoreType.REGULAR,
+                pltpu.SemaphoreType.REGULAR((3 + others,)),
             ],
             compiler_params=pltpu.CompilerParams(
                 collective_id=0, has_side_effects=True, vmem_limit_bytes=room

time: 46.8 us -> 45.7 us (0.976)
  Pallas kernels: 46 us -> 44.8 us
    pallas_call x1, Pallas kernels: 45 us -> 43.8 us  [local(): pl.pallas_call(functools.partial(kernel, blocks, lanes), out_shape=(vmem(...]
where the time goes in v6:
time: 45.7 us; the launch traced here: 45.4 us
  Pallas kernels  44.8 us (98%)
  between operations  0.64 us (1%)
    pallas_call x1, Pallas kernels, local(): pl.pallas_call(functools.partial(kernel, blocks, lanes), out_shape=(vmem(...  43.8 us
    pallas_call x1, Pallas kernels, local(): pl.pallas_call(place, out_shape=shapes, in_specs=[here] * 2, out_specs=(h...  0.99 us

profile of v6, /device:TPU:0, one launch (start us, length us, event | category | flops | bytes accessed | tf_op | source)
XLA Modules:
  0.0 45.4 jit_solution(7544716886783555860)
XLA Ops:
  0.6 43.8 %shard_map.68 = (bf16[512,512]{1,0:T(8,128)(2,1)S(1)}, bf16[1,512,512]{2,1,0:T(8,128)(2,1)S(1)}) custom-call(bf16[512,512]{1,0:T(8,128)(2,1)} %left_hbm.1, bf16[1,512,512]{2,1,0:T(8,128)(2,1)} %right_hbm.1, bf16[1,4,512,512]{3,2,1,0:T(8,128)(2,1)} %obs_hbm.1, s32[1,512]{1,0:T(1,128)} %bitcast.1, s32[1,4,512]{2,1,0:T(4,128)} %shift_hbm.1), custom_call_target="tpu_custom_call" | custom-call | tf_op jit(solution)/shard_map/pallas_call | solution.py:468
  44.5 1.0 %shard_map.69 = (bf16[512,512]{1,0:T(8,128)(2,1)}, bf16[1,512,512]{2,1,0:T(8,128)(2,1)}) custom-call(bf16[512,512]{1,0:T(8,128)(2,1)S(1)} %get-tuple-element.4.left_from, bf16[1,512,512]{2,1,0:T(8,128)(2,1)S(1)} %get-tuple-element.5.right_from), custom_call_target="tpu_custom_call" | custom-call | tf_op jit(solution)/shard_map/pallas_call | solution.py:517

commit v7 on v6

--- a/solution.py
+++ b/solution.py
@@ -12,10 +12,7 @@
 step_left = 0.1
 
 CHUNKS = 8
-LAG = 5
-HOLD = 1
-EARLY = 2
-RETURN = 5
+PAIRS = CHUNKS // 2
 WIDTH = 128
 PIECES = 8
 SUBS = 2
@@ -41,7 +38,7 @@
     rank = left.shape[1]
     scale = 1.0 / math.sqrt(rank)
     size = cols // CHUNKS
-    ready = cols - EARLY * size
+    early = cols - size
     half = rows // 2
     part = half // PIECES
     own = rows // lanes
@@ -97,8 +94,8 @@
             device_id=place, device_id_type=MESH,
         )
 
-    def chunk(k):
-        return pl.ds(pl.multiple_of(k * size, size), size)
+    def chunk(k, count=1):
+        return pl.ds(pl.multiple_of(k * size, size), count * size)
 
     natural = [s for s in range(steps) if s != GUEST]
     loads = [
@@ -127,19 +124,14 @@
         span = piece(lane if m == 0 else sources[m - 1], u)
         return remote(left_g.at[span], left_g.at[span], pair_share_send.at[m], pair_share_recv.at[m, u], lane=pair)
 
-    def given(k):
-        span = chunk(k)
-        return remote(obs_hbm.at[0, GUEST, span], obs_g.at[span], tile_send.at[0], tile_recv.at[k], blk=partner)
-
-    def give_sent(late):
-        span = pl.ds(ready, cols - ready) if late else pl.ds(0, ready)
-        return remote(obs_hbm.at[0, GUEST, span], obs_g.at[span], tile_send.at[late], tile_recv.at[0], blk=partner)
-
-    def give(k):
-        span = chunk(k)
-        return remote(
-            obs_hbm.at[0, GUEST, span], obs_g.at[span], tile_send.at[int(k >= CHUNKS - EARLY)], tile_recv.at[k], blk=partner
-        )
+    def give(p, group=0):
+        span = chunk(2 * p, 2)
+        return remote(obs_hbm.at[0, GUEST, span], obs_g.at[span], tile_send.at[group], tile_recv.at[p], blk=partner)
+
+    def give_sent(group):
+        first_col = (0, cols - 4 * size, cols - 2 * size)[group]
+        span = pl.ds(first_col, cols - 4 * size if group == 0 else 2 * size)
+        return remote(obs_hbm.at[0, GUEST, span], obs_g.at[span], tile_send.at[group], tile_recv.at[0], blk=partner)
 
     tables = [
         remote(codes_hbm, codes_g, table_send.at[0], table_recv.at[0], blk=partner),
@@ -159,8 +151,7 @@
             span = pl.ds(start, width)
             turned[s, span, :] = jnp.transpose(jnp.broadcast_to(table[0, pl.ds(s, 1), span], (width, width)))
 
-    def error_of(k, s, block, factor, words, target):
-        span = chunk(k)
+    def error_of(span, s, block, factor, words, target):
         shifts = jnp.concatenate([turned[s, span, :]] * (rows // width), axis=1)
         seen = (jnp.right_shift(words[...], shifts) & 1) == 1
         predicted = lax.dot_general(
@@ -173,41 +164,53 @@
         move = jnp.dot(error, factor[...], preferred_element_type=jnp.float32)
         return (block.astype(jnp.float32) - step_right * scale * move).astype(jnp.bfloat16)
 
-    def tile(k, s, source, target, guest=False):
-        span = chunk(k)
+    def tile(k, s, source, target, guest=False, count=1):
+        span = chunk(k, count)
         block = source[span, :]
         if guest:
             factor, words, wanted = left_g, codes_g, obs_g
         else:
             factor, words, wanted = left, codes, obs.at[natural.index(s)]
-        error = error_of(k, s, block, factor, words, wanted)
+        error = error_of(span, s, block, factor, words, wanted)
         errs[s, span, :] = error
         target[span, :] = stepped(error, block, factor)
 
     last = steps - 1
 
-    def last_visit(k):
-        cross_over(k).wait_recv()
-        tile(k, last, turn_in, final)
+    def last_visit(k, count=1):
+        for step in range(count):
+            cross_over(k + step).wait_recv()
+        tile(k, last, turn_in, final, count=count)
+
+    def last_pair(p):
+        last_visit(2 * p, 2)
 
     def outer(error, block):
         return lax.dot_general(error, block, (((0,), (0,)), ((), ())), preferred_element_type=jnp.float32)
 
-    loads[0].wait()
-    turn(0, shift)
+    def open_table():
+        loads[0].wait()
+        turn(0, shift)
+
     pl.semaphore_wait(barrier, greeters)
     pl.when(odd == 1)(lambda: answer(0, blk=partner))
     pl.when((odd == 0) & inner_blk)(lambda: answer(1, blk=behind))
     pl.when(inner_blk)(lambda: answer(2, blk=behind2))
     for m, peer in enumerate(peers):
         pl.when(peer < lane)(functools.partial(answer, 3 + others - 1 - m, lane=peer))
-    pl.when(odd == 0)(lambda: await_answer(0))
+
+    @pl.when(odd == 0)
+    def _():
+        open_table()
+        await_answer(0)
+
     for u in range(SUBS):
         lend(u).start()
     for copy in tables:
         copy.start()
-    for k in range(CHUNKS):
-        give(k).start()
+    for p in range(PAIRS):
+        give(p, max(0, p + 3 - PAIRS)).start()
+    pl.when(odd == 1)(open_table)
     for copy in loads[1:5]:
         copy.wait()
 
@@ -272,10 +275,11 @@
 
         pl.when(~wraps)(lambda: await_answer(2))
 
-        def guest_visit(k):
-            given(k).wait_recv()
-            tile(k, GUEST, inner, hop_out, guest=True)
-            hop(k).start()
+        def guest_pair(p):
+            give(p).wait_recv()
+            tile(2 * p, GUEST, inner, hop_out, guest=True, count=2)
+            for step in range(2):
+                hop(2 * p + step).start()
 
         def home_visit(k):
             hop(k).wait_recv()
@@ -284,28 +288,26 @@
 
         loads[5].wait()
         loads[6].wait()
-        pl.loop(0, LAG)(guest_visit)
+        pl.loop(0, PAIRS - 1)(guest_pair)
         give_sent(0).wait_send()
         give_sent(1).wait_send()
         pl.semaphore_signal(clear_sem, inc=1, device_id={"lane": pair}, device_id_type=MESH)
         pl.semaphore_wait(clear_sem, 1)
-
-        @pl.loop(LAG, CHUNKS)
-        def _(k):
-            home_visit(k - LAG)
-            guest_visit(k)
-
+        pl.loop(0, PAIRS - 1)(home_visit)
+        guest_pair(PAIRS - 1)
         grad_g[...] = outer(errs[GUEST], inner[...])
         send_back()
-        pl.loop(CHUNKS - LAG, CHUNKS - LAG + 2)(home_visit)
+        pl.loop(PAIRS - 1, PAIRS + 1)(home_visit)
         send_fold()
 
-        @pl.loop(CHUNKS - LAG + 2, CHUNKS)
-        def _(k):
-            home_visit(k)
-            last_visit(k - (CHUNKS - LAG + 2))
-
-        grad[...] += outer(errs[2], hop_in[...])
+        pl.loop(PAIRS + 1, CHUNKS - 1)(home_visit)
+        last_pair(0)
+        before, after = pl.ds(0, early), pl.ds(early, size)
+        grad[...] += outer(errs[2, before], hop_in[before])
+        home_visit(CHUNKS - 1)
+        last_pair(1)
+        grad[...] += outer(errs[2, after], hop_in[after])
+        give_sent(2).wait_send()
 
     @pl.when(odd == 1)
     def _():
@@ -326,49 +328,74 @@
         loads[5].wait()
         loads[6].wait()
 
-        def visits(k):
-            given(k).wait_recv()
-            hop(k).wait_recv()
-            tile(k, GUEST, hop_in, inner, guest=True)
-            tile(k, 2, inner, turn_out)
-
-        pl.loop(0, HOLD)(visits)
-        give_sent(0).wait_send()
-        pl.semaphore_signal(clear_sem, inc=1, device_id={"lane": pair}, device_id_type=MESH)
-        pl.semaphore_wait(clear_sem, 1)
-        pl.semaphore_signal(go_sem, inc=1, device_id={"blk": behind2}, device_id_type=MESH)
-        pl.semaphore_wait(go_sem, 1)
-        pl.when(~ends)(lambda: await_answer(1))
-        pl.loop(0, HOLD)(lambda k: cross_over(k).start())
-
-        @pl.loop(HOLD, CHUNKS)
-        def _(k):
-            visits(k)
-            cross_over(k).start()
+        def visit_pair(p):
+            give(p).wait_recv()
+            for step in range(2):
+                hop(2 * p + step).wait_recv()
+            tile(2 * p, GUEST, hop_in, inner, guest=True, count=2)
+            tile(2 * p, 2, inner, turn_out, count=2)
+
+        def send_pair(p):
+            for step in range(2):
+                cross_over(2 * p + step).start()
+
+        def release(*groups):
+            for group in groups:
+                give_sent(group).wait_send()
+            pl.semaphore_signal(clear_sem, inc=1, device_id={"lane": pair}, device_id_type=MESH)
+            pl.semaphore_wait(clear_sem, 1)
+            pl.semaphore_signal(go_sem, inc=1, device_id={"blk": behind2}, device_id_type=MESH)
+
+        def go():
+            pl.semaphore_wait(go_sem, 1)
+            pl.when(~ends)(lambda: await_answer(1))
+            send_pair(0)
+
+        visit_pair(0)
+
+        @pl.when(blk == 1)
+        def _():
+            release(0)
+            go()
+            give_sent(1).wait_send()
+
+        @pl.when((blk > 1) & ~wraps)
+        def _():
+            release(0, 1)
+            go()
+
+        @pl.when((blk > 1) & wraps)
+        def _():
+            go()
+            release(0, 1)
+
+        @pl.loop(1, PAIRS)
+        def _(p):
+            visit_pair(p)
+            send_pair(p)
 
         grad_g[...] = outer(errs[GUEST], hop_in[...])
         send_back()
         grad[...] += outer(errs[2], inner[...])
-        give_sent(1).wait_send()
+        give_sent(2).wait_send()
         send_fold()
 
-    pl.loop(lax.select(odd == 0, LAG - 2, 0), RETURN)(last_visit)
+    pl.loop(2 - 2 * odd, CHUNKS // 2 - 1)(last_pair)
     send_return()
-    pl.loop(RETURN, CHUNKS - 1)(last_visit)
-
-    early = (CHUNKS - 1) * size
+    last_visit(CHUNKS - 2)
+
     grad[...] += outer(errs[last, pl.ds(0, early)], turn_in[pl.ds(0, early)])
     tail = pl.ds(early, size)
     cross_over(CHUNKS - 1).wait_recv()
-    errs[last, tail, :] = error_of(CHUNKS - 1, last, turn_in[tail, :], left, codes, obs.at[natural.index(last)])
+    errs[last, tail, :] = error_of(tail, last, turn_in[tail, :], left, codes, obs.at[natural.index(last)])
 
     def finish(start):
         span = pl.ds(pl.multiple_of(start, width), width)
         return grad[span, :] + outer(errs[last, tail, span], turn_in[tail, :])
 
-    def swap(q):
-        span = pl.ds(pl.multiple_of(q * part, part), part)
-        return remote(pair_out.at[span], pair_in.at[span], swap_send.at[0], swap_recv.at[q], lane=pair)
+    def swap(start):
+        span = pl.ds(pl.multiple_of(start, width), width)
+        return remote(pair_out.at[span], pair_in.at[span], swap_send.at[0], swap_recv.at[start // width], lane=pair)
 
     def cross(m, n):
         span = pl.ds(pl.multiple_of(n * part, part), part)
@@ -378,16 +405,17 @@
         span = pl.ds(pl.multiple_of(mine + n * part, part), part)
         return remote(result.at[span], result.at[span], last_send.at[0], last_recv.at[0], lane=pair)
 
-    for start in range(0, half, width):
-        pair_out[pl.ds(start, width), :] = finish(other + start).astype(jnp.bfloat16)
-        for q in range(start // part, (start + width) // part):
-            swap(q).start()
-    for start in range(0, half, width):
+    starts = [lax.rem((chip + 1) * own + step, half) for step in range(0, half, width)]
+    for start in starts:
+        pair_out[pl.ds(pl.multiple_of(start, width), width), :] = finish(other + start).astype(jnp.bfloat16)
+        swap(start).start()
+    for start in starts:
         grad[pl.ds(pl.multiple_of(mine + start, width), width), :] = finish(mine + start)
     for q in range(PIECES):
         n = lax.rem((chip + 1) * quota + q, PIECES)
         span = pl.ds(pl.multiple_of(n * part, part), part)
-        swap(n).wait_recv()
+        if q % (width // part) == 0:
+            swap(n * part).wait_recv()
         total = (
             grad[pl.ds(pl.multiple_of(mine + n * part, part), part), :]
             + pair_in[span, :].astype(jnp.float32)
@@ -490,7 +518,7 @@
                 *[vmem((half, rank), bf16)] * 3,
                 vmem((others, half, rank), bf16),
                 dma((4 + steps - 1,)),
-                dma((2,)), dma((CHUNKS,)),
+                dma((3,)), dma((PAIRS,)),
                 dma((2,)), dma((2,)),
                 dma((1,)), dma((SUBS,)),
                 dma((others,)), dma((others, SUBS)),
@@ -499,8 +527,8 @@
                 dma((1,)), dma((CHUNKS,)),
                 dma((1,)), dma((1,)),
                 dma((others,)), dma((others,)),
-                dma((1,)), dma((PIECES,)),
-                dma((1,)), dma((PIECES,)),
+                dma((1,)), dma((PIECES * 2 // lanes,)),
+                dma((1,)), dma((half // WIDTH,)),
                 dma((others,)), dma((others, PIECES)),
                 dma((1,)), dma((1,)),
                 pltpu.SemaphoreType.REGULAR,

time: 45.7 us -> 44.3 us (0.969)
  Pallas kernels: 44.8 us -> 43.4 us
    pallas_call x1, Pallas kernels: 43.8 us -> 42.4 us  [local(): pl.pallas_call(functools.partial(kernel, blocks, lanes), out_shape=(vmem(...]
where the time goes in v7:
time: 44.3 us; the launch traced here: 44.1 us
  Pallas kernels  43.4 us (98%)
  between operations  0.64 us (1%)
    pallas_call x1, Pallas kernels, local(): pl.pallas_call(functools.partial(kernel, blocks, lanes), out_shape=(vmem(...  42.4 us
    pallas_call x1, Pallas kernels, local(): pl.pallas_call(place, out_shape=shapes, in_specs=[here] * 2, out_specs=(h...  0.99 us

profile of v7, /device:TPU:0, one launch (start us, length us, event | category | flops | bytes accessed | tf_op | source)
XLA Modules:
  0.0 44.1 jit_solution(11244130211198810293)
XLA Ops:
  0.6 42.4 %shard_map.68 = (bf16[512,512]{1,0:T(8,128)(2,1)S(1)}, bf16[1,512,512]{2,1,0:T(8,128)(2,1)S(1)}) custom-call(bf16[512,512]{1,0:T(8,128)(2,1)} %left_hbm.1, bf16[1,512,512]{2,1,0:T(8,128)(2,1)} %right_hbm.1, bf16[1,4,512,512]{3,2,1,0:T(8,128)(2,1)} %obs_hbm.1, s32[1,512]{1,0:T(1,128)} %bitcast.1, s32[1,4,512]{2,1,0:T(4,128)} %shift_hbm.1), custom_call_target="tpu_custom_call" | custom-call | tf_op jit(solution)/shard_map/pallas_call | solution.py:496
  43.1 1.0 %shard_map.69 = (bf16[512,512]{1,0:T(8,128)(2,1)}, bf16[1,512,512]{2,1,0:T(8,128)(2,1)}) custom-call(bf16[512,512]{1,0:T(8,128)(2,1)S(1)} %get-tuple-element.4.left_from, bf16[1,512,512]{2,1,0:T(8,128)(2,1)S(1)} %get-tuple-element.5.right_from), custom_call_target="tpu_custom_call" | custom-call | tf_op jit(solution)/shard_map/pallas_call | solution.py:545

commit v8 on v7

--- a/solution.py
+++ b/solution.py
@@ -14,7 +14,7 @@
 CHUNKS = 8
 PAIRS = CHUNKS // 2
 WIDTH = 128
-PIECES = 8
+PIECES = 4
 SUBS = 2
 GUEST = 1
 VMEM_BYTES = 67043328
@@ -104,9 +104,10 @@
         pltpu.make_async_copy(right_hbm.at[0], first, load_sem.at[2]),
         pltpu.make_async_copy(left_hbm, left, load_sem.at[3]),
     ]
-    for n, s in enumerate(natural):
-        loads.append(pltpu.make_async_copy(obs_hbm.at[0, s], obs.at[n], load_sem.at[4 + n]))
-    for copy in loads:
+    later = pl.ds(GUEST + 1, steps - 1 - GUEST)
+    loads.append(pltpu.make_async_copy(obs_hbm.at[0, 0], obs.at[0], load_sem.at[4]))
+    loads.append(pltpu.make_async_copy(obs_hbm.at[0, later], obs.at[pl.ds(1, steps - 2)], load_sem.at[5]))
+    for copy in loads[:5]:
         copy.start()
 
     def piece(owner, u):
@@ -142,9 +143,9 @@
         span = chunk(k)
         return remote(hop_out.at[span], hop_in.at[span], hop_send.at[0], hop_recv.at[k], blk=ahead2)
 
-    def cross_over(k):
-        span = chunk(k)
-        return remote(turn_out.at[span], turn_in.at[span], turn_send.at[0], turn_recv.at[k], blk=ahead)
+    def cross_over(k, count=1):
+        span = chunk(k, count)
+        return remote(turn_out.at[span], turn_in.at[span], turn_send.at[0], turn_recv.at[k // 2 + k // (CHUNKS - 1)], blk=ahead)
 
     def turn(s, table):
         for start in range(0, cols, width):
@@ -178,8 +179,7 @@
     last = steps - 1
 
     def last_visit(k, count=1):
-        for step in range(count):
-            cross_over(k + step).wait_recv()
+        cross_over(k, count).wait_recv()
         tile(k, last, turn_in, final, count=count)
 
     def last_pair(p):
@@ -213,6 +213,8 @@
     pl.when(odd == 1)(open_table)
     for copy in loads[1:5]:
         copy.wait()
+    for copy in loads[5:]:
+        copy.start()
 
     def relay():
         for m, peer in enumerate(peers):
@@ -266,7 +268,7 @@
 
     @pl.when(odd == 0)
     def _():
-        pl.loop(0, CHUNKS)(lambda k: tile(k, 0, first, inner))
+        pl.loop(0, PAIRS)(lambda p: tile(2 * p, 0, first, inner, count=2))
         relay()
         grad[...] = outer(errs[0], first[...])
         turn(2, shift)
@@ -287,7 +289,6 @@
             cross_over(k).start()
 
         loads[5].wait()
-        loads[6].wait()
         pl.loop(0, PAIRS - 1)(guest_pair)
         give_sent(0).wait_send()
         give_sent(1).wait_send()
@@ -300,25 +301,31 @@
         pl.loop(PAIRS - 1, PAIRS + 1)(home_visit)
         send_fold()
 
-        pl.loop(PAIRS + 1, CHUNKS - 1)(home_visit)
+        pl.loop(PAIRS + 1, CHUNKS - 2)(home_visit)
         last_pair(0)
-        before, after = pl.ds(0, early), pl.ds(early, size)
-        grad[...] += outer(errs[2, before], hop_in[before])
+        home_visit(CHUNKS - 2)
+        last_pair(1)
         home_visit(CHUNKS - 1)
-        last_pair(1)
-        grad[...] += outer(errs[2, after], hop_in[after])
+        grad[...] += outer(errs[2], hop_in[...])
         give_sent(2).wait_send()
 
     @pl.when(odd == 1)
     def _():
-        tile(0, 0, first, hop_out)
+        def start_pair(p):
+            tile(2 * p, 0, first, hop_out, count=2)
+
+        def hop_pair(p):
+            for step in range(2):
+                hop(2 * p + step).start()
+
+        start_pair(0)
         pl.when(~wraps)(lambda: await_answer(2))
-        hop(0).start()
-
-        @pl.loop(1, CHUNKS)
-        def _(k):
-            tile(k, 0, first, hop_out)
-            hop(k).start()
+        hop_pair(0)
+
+        @pl.loop(1, PAIRS)
+        def _(p):
+            start_pair(p)
+            hop_pair(p)
 
         relay()
         grad[...] = outer(errs[0], first[...])
@@ -326,7 +333,6 @@
         turn(3, shift)
         gather()
         loads[5].wait()
-        loads[6].wait()
 
         def visit_pair(p):
             give(p).wait_recv()
@@ -382,9 +388,11 @@
 
     pl.loop(2 - 2 * odd, CHUNKS // 2 - 1)(last_pair)
     send_return()
+    grad[...] += outer(errs[last, pl.ds(0, cols - 4 * size)], turn_in[pl.ds(0, cols - 4 * size)])
     last_visit(CHUNKS - 2)
 
-    grad[...] += outer(errs[last, pl.ds(0, early)], turn_in[pl.ds(0, early)])
+    rest = pl.ds(cols - 4 * size, 3 * size)
+    grad[...] += outer(errs[last, rest], turn_in[rest])
     tail = pl.ds(early, size)
     cross_over(CHUNKS - 1).wait_recv()
     errs[last, tail, :] = error_of(tail, last, turn_in[tail, :], left, codes, obs.at[natural.index(last)])
@@ -517,14 +525,14 @@
                 *[vmem((rows // lanes, rank), bf16)] * 2,
                 *[vmem((half, rank), bf16)] * 3,
                 vmem((others, half, rank), bf16),
-                dma((4 + steps - 1,)),
+                dma((6,)),
                 dma((3,)), dma((PAIRS,)),
                 dma((2,)), dma((2,)),
                 dma((1,)), dma((SUBS,)),
                 dma((others,)), dma((others, SUBS)),
                 dma((1 + others,)), dma((1 + others, SUBS)),
                 dma((1,)), dma((CHUNKS,)),
-                dma((1,)), dma((CHUNKS,)),
+                dma((1,)), dma((PAIRS + 1,)),
                 dma((1,)), dma((1,)),
                 dma((others,)), dma((others,)),
                 dma((1,)), dma((PIECES * 2 // lanes,)),

time: 44.3 us -> 44 us (level)
  no operation moved by 1% of the time
where the time goes in v8:
time: 44 us; the launch traced here: 43.8 us
  Pallas kernels  43.2 us (98%)
  between operations  0.64 us (1%)
    pallas_call x1, Pallas kernels, local(): pl.pallas_call(functools.partial(kernel, blocks, lanes), out_shape=(vmem(...  42.2 us
    pallas_call x1, Pallas kernels, local(): pl.pallas_call(place, out_shape=shapes, in_specs=[here] * 2, out_specs=(h...  0.99 us

profile of v8, /device:TPU:0, one launch (start us, length us, event | category | flops | bytes accessed | tf_op | source)
XLA Modules:
  0.0 43.8 jit_solution(11476646169615159626)
XLA Ops:
  0.6 42.2 %shard_map.68 = (bf16[512,512]{1,0:T(8,128)(2,1)S(1)}, bf16[1,512,512]{2,1,0:T(8,128)(2,1)S(1)}) custom-call(bf16[512,512]{1,0:T(8,128)(2,1)} %left_hbm.1, bf16[1,512,512]{2,1,0:T(8,128)(2,1)} %right_hbm.1, bf16[1,4,512,512]{3,2,1,0:T(8,128)(2,1)} %obs_hbm.1, s32[1,512]{1,0:T(1,128)} %bitcast.1, s32[1,4,512]{2,1,0:T(4,128)} %shift_hbm.1), custom_call_target="tpu_custom_call" | custom-call | tf_op jit(solution)/shard_map/pallas_call | solution.py:504
  42.8 1.0 %shard_map.69 = (bf16[512,512]{1,0:T(8,128)(2,1)}, bf16[1,512,512]{2,1,0:T(8,128)(2,1)}) custom-call(bf16[512,512]{1,0:T(8,128)(2,1)S(1)} %get-tuple-element.4.left_from, bf16[1,512,512]{2,1,0:T(8,128)(2,1)S(1)} %get-tuple-element.5.right_from), custom_call_target="tpu_custom_call" | custom-call | tf_op jit(solution)/shard_map/pallas_call | solution.py:553

commit v9 on v8

--- a/solution.py
+++ b/solution.py
@@ -291,7 +291,6 @@
         loads[5].wait()
         pl.loop(0, PAIRS - 1)(guest_pair)
         give_sent(0).wait_send()
-        give_sent(1).wait_send()
         pl.semaphore_signal(clear_sem, inc=1, device_id={"lane": pair}, device_id_type=MESH)
         pl.semaphore_wait(clear_sem, 1)
         pl.loop(0, PAIRS - 1)(home_visit)
@@ -307,6 +306,7 @@
         last_pair(1)
         home_visit(CHUNKS - 1)
         grad[...] += outer(errs[2], hop_in[...])
+        give_sent(1).wait_send()
         give_sent(2).wait_send()
 
     @pl.when(odd == 1)

time: 44 us -> 44 us (level)
  no operation moved by 1% of the time
where the time goes in v9:
time: 44 us; the launch traced here: 43.8 us
  Pallas kernels  43.2 us (98%)
  between operations  0.64 us (1%)
    pallas_call x1, Pallas kernels, local(): pl.pallas_call(functools.partial(kernel, blocks, lanes), out_shape=(vmem(...  42.2 us
    pallas_call x1, Pallas kernels, local(): pl.pallas_call(place, out_shape=shapes, in_specs=[here] * 2, out_specs=(h...  0.99 us

profile of v9, /device:TPU:0, one launch (start us, length us, event | category | flops | bytes accessed | tf_op | source)
XLA Modules:
  0.0 43.8 jit_solution(17862007351681453423)
XLA Ops:
  0.6 42.2 %shard_map.68 = (bf16[512,512]{1,0:T(8,128)(2,1)S(1)}, bf16[1,512,512]{2,1,0:T(8,128)(2,1)S(1)}) custom-call(bf16[512,512]{1,0:T(8,128)(2,1)} %left_hbm.1, bf16[1,512,512]{2,1,0:T(8,128)(2,1)} %right_hbm.1, bf16[1,4,512,512]{3,2,1,0:T(8,128)(2,1)} %obs_hbm.1, s32[1,512]{1,0:T(1,128)} %bitcast.1, s32[1,4,512]{2,1,0:T(4,128)} %shift_hbm.1), custom_call_target="tpu_custom_call" | custom-call | tf_op jit(solution)/shard_map/pallas_call | solution.py:504
  42.8 1.0 %shard_map.69 = (bf16[512,512]{1,0:T(8,128)(2,1)}, bf16[1,512,512]{2,1,0:T(8,128)(2,1)}) custom-call(bf16[512,512]{1,0:T(8,128)(2,1)S(1)} %get-tuple-element.4.left_from, bf16[1,512,512]{2,1,0:T(8,128)(2,1)S(1)} %get-tuple-element.5.right_from), custom_call_target="tpu_custom_call" | custom-call | tf_op jit(solution)/shard_map/pallas_call | solution.py:553

commit v10 on v8

--- a/solution.py
+++ b/solution.py
@@ -15,7 +15,7 @@
 PAIRS = CHUNKS // 2
 WIDTH = 128
 PIECES = 4
-SUBS = 2
+SUBS = 4
 GUEST = 1
 VMEM_BYTES = 67043328
 MESH = pl.DeviceIdType.MESH
@@ -123,7 +123,7 @@
 
     def lend_pair(m, u):
         span = piece(lane if m == 0 else sources[m - 1], u)
-        return remote(left_g.at[span], left_g.at[span], pair_share_send.at[m], pair_share_recv.at[m, u], lane=pair)
+        return remote(left_g.at[span], left_g.at[span], pair_share_send.at[0], pair_share_recv.at[0], lane=pair)
 
     def give(p, group=0):
         span = chunk(2 * p, 2)
@@ -225,6 +225,9 @@
                 lend_peer(m, u).start()
             lend_pair(0, u).start()
 
+    passed = left_g.at[pl.ds(0, (1 + others) * own)]
+    lent_pair = remote(passed, passed, pair_share_send.at[0], pair_share_recv.at[0], lane=pair)
+
     def gather():
         for u in range(SUBS):
             for m in range(others):
@@ -233,9 +236,7 @@
         for copy in tables:
             copy.wait_recv()
         turn(GUEST, shift_g)
-        for m in range(1 + others):
-            for u in range(SUBS):
-                lend_pair(m, u).wait_recv()
+        lent_pair.wait_recv()
 
     back = remote(back_out, back_in, back_send.at[0], back_recv.at[0], lane=pair)
 
@@ -442,8 +443,7 @@
     remote(left_hbm.at[lent], left_g.at[lent], share_send.at[0], share_recv.at[0], blk=partner).wait_send()
     for m in range(others):
         remote(left_g.at[lent], left_g.at[lent], peer_share_send.at[m], peer_share_recv.at[m, 0], lane=peers[m]).wait_send()
-    for m in range(1 + others):
-        remote(left_g.at[lent], left_g.at[lent], pair_share_send.at[m], pair_share_recv.at[m, 0], lane=pair).wait_send()
+    lent_pair.wait_send()
     for copy in tables:
         copy.wait_send()
     remote(hop_out, hop_in, hop_send.at[0], hop_recv.at[0], blk=ahead2).wait_send()
@@ -530,7 +530,7 @@
                 dma((2,)), dma((2,)),
                 dma((1,)), dma((SUBS,)),
                 dma((others,)), dma((others, SUBS)),
-                dma((1 + others,)), dma((1 + others, SUBS)),
+                dma((1,)), dma((1,)),
                 dma((1,)), dma((CHUNKS,)),
                 dma((1,)), dma((PAIRS + 1,)),
                 dma((1,)), dma((1,)),

time: 44 us -> 44 us (level)
  no operation moved by 1% of the time
where the time goes in v10:
time: 44 us; the launch traced here: 43.8 us
  Pallas kernels  43.1 us (98%)
  between operations  0.64 us (1%)
    pallas_call x1, Pallas kernels, local(): pl.pallas_call(functools.partial(kernel, blocks, lanes), out_shape=(vmem(...  42.2 us
    pallas_call x1, Pallas kernels, local(): pl.pallas_call(place, out_shape=shapes, in_specs=[here] * 2, out_specs=(h...  0.99 us

profile of v10, /device:TPU:0, one launch (start us, length us, event | category | flops | bytes accessed | tf_op | source)
XLA Modules:
  0.0 43.8 jit_solution(701352464656475271)
XLA Ops:
  0.6 42.2 %shard_map.68 = (bf16[512,512]{1,0:T(8,128)(2,1)S(1)}, bf16[1,512,512]{2,1,0:T(8,128)(2,1)S(1)}) custom-call(bf16[512,512]{1,0:T(8,128)(2,1)} %left_hbm.1, bf16[1,512,512]{2,1,0:T(8,128)(2,1)} %right_hbm.1, bf16[1,4,512,512]{3,2,1,0:T(8,128)(2,1)} %obs_hbm.1, s32[1,512]{1,0:T(1,128)} %bitcast.1, s32[1,4,512]{2,1,0:T(4,128)} %shift_hbm.1), custom_call_target="tpu_custom_call" | custom-call | tf_op jit(solution)/shard_map/pallas_call | solution.py:504
  42.8 1.0 %shard_map.69 = (bf16[512,512]{1,0:T(8,128)(2,1)}, bf16[1,512,512]{2,1,0:T(8,128)(2,1)}) custom-call(bf16[512,512]{1,0:T(8,128)(2,1)S(1)} %get-tuple-element.4.left_from, bf16[1,512,512]{2,1,0:T(8,128)(2,1)S(1)} %get-tuple-element.5.right_from), custom_call_target="tpu_custom_call" | custom-call | tf_op jit(solution)/shard_map/pallas_call | solution.py:553

commit v11 on v10

--- a/solution.py
+++ b/solution.py
@@ -292,7 +292,6 @@
         loads[5].wait()
         pl.loop(0, PAIRS - 1)(guest_pair)
         give_sent(0).wait_send()
-        give_sent(1).wait_send()
         pl.semaphore_signal(clear_sem, inc=1, device_id={"lane": pair}, device_id_type=MESH)
         pl.semaphore_wait(clear_sem, 1)
         pl.loop(0, PAIRS - 1)(home_visit)
@@ -308,6 +307,7 @@
         last_pair(1)
         home_visit(CHUNKS - 1)
         grad[...] += outer(errs[2], hop_in[...])
+        give_sent(1).wait_send()
         give_sent(2).wait_send()
 
     @pl.when(odd == 1)

time: 44 us -> 44 us (level)
  no operation moved by 1% of the time
where the time goes in v11:
time: 44 us; the launch traced here: 43.8 us
  Pallas kernels  43.1 us (98%)
  between operations  0.64 us (1%)
    pallas_call x1, Pallas kernels, local(): pl.pallas_call(functools.partial(kernel, blocks, lanes), out_shape=(vmem(...  42.2 us
    pallas_call x1, Pallas kernels, local(): pl.pallas_call(place, out_shape=shapes, in_specs=[here] * 2, out_specs=(h...  0.99 us

profile of v11, /device:TPU:0, one launch (start us, length us, event | category | flops | bytes accessed | tf_op | source)
XLA Modules:
  0.0 43.8 jit_solution(12971670782014601922)
XLA Ops:
  0.6 42.2 %shard_map.68 = (bf16[512,512]{1,0:T(8,128)(2,1)S(1)}, bf16[1,512,512]{2,1,0:T(8,128)(2,1)S(1)}) custom-call(bf16[512,512]{1,0:T(8,128)(2,1)} %left_hbm.1, bf16[1,512,512]{2,1,0:T(8,128)(2,1)} %right_hbm.1, bf16[1,4,512,512]{3,2,1,0:T(8,128)(2,1)} %obs_hbm.1, s32[1,512]{1,0:T(1,128)} %bitcast.1, s32[1,4,512]{2,1,0:T(4,128)} %shift_hbm.1), custom_call_target="tpu_custom_call" | custom-call | tf_op jit(solution)/shard_map/pallas_call | solution.py:504
  42.8 1.0 %shard_map.69 = (bf16[512,512]{1,0:T(8,128)(2,1)}, bf16[1,512,512]{2,1,0:T(8,128)(2,1)}) custom-call(bf16[512,512]{1,0:T(8,128)(2,1)S(1)} %get-tuple-element.4.left_from, bf16[1,512,512]{2,1,0:T(8,128)(2,1)S(1)} %get-tuple-element.5.right_from), custom_call_target="tpu_custom_call" | custom-call | tf_op jit(solution)/shard_map/pallas_call | solution.py:553
